TPU v7x, 32 devices: a whole 2x2x4 slice. The times are simulated.
32 devices in a mesh: band: 4 (over z), ga: 8 (over y, x, core).
Axes of the slice: x: 2, y: 2, z: 4, core: 2. Of those that a mesh axis runs over, the one named last changes fastest.
Arguments:
- coeffs: float32 [2, 4, 18432], P(None, 'band', 'ga'), may hold values from -8 to 8
- cell_map: int32 [18432], P('ga'), may hold values from 0 to 110591, as said below
- potential: float32 [96, 96, 96], P(None, 'ga'), may hold values from -2 to 1
- projectors: float32 [2, 64, 18432], P(None, None, 'ga'), may hold values from -6 to 6
- strengths: float32 [8, 8, 8], replicated, may hold values from -2 to 2
- proj_atom: int32 [64], replicated, may hold values from 0 to 7, as said below
- proj_chan: int32 [64], replicated, may hold values from 0 to 7, as said below
Outputs:
- new_bands: float32 [2, 4, 18432], P(None, 'band', 'ga')
- energy: float32 [4], P('band')
- residual_norm: float32 [4], P('band')
- correlation: float32 [2, 4, 4], P(None, 'band')
- subspace: float32 [2, 4, 4], P(None, 'band')
Inputs may be any that keep to these rules, and one draw needn't show every extreme that they name: `cell_map`: in block d (entries d * 2304 to (d + 1) * 2304 - 1) the entries are distinct cells (i * 96 + y) * 96 + z of grid planes x = d + 8 * i. `proj_atom`: each pair of atom and channel belongs to exactly one projector. `proj_chan`: each pair of atom and channel belongs to exactly one projector.
All inputs are finite; a program needn't handle non-finite values.
Results may differ from a plain program's by a relative error of at most 0.0002.
Values sent between devices are 32-bit elements; how exact they have to be, the bound alone decides.
A program may use at most 64 MiB of HBM per device.

v0:
```python
import jax
import jax.numpy as jnp
from jax import lax
from jax.sharding import PartitionSpec as P

top_precision = lax.Precision.HIGHEST
kin_unit = 0.02
small_eps = 1e-06


def signed_freq(index_arr, grid_len):
    return jnp.where(index_arr < grid_len // 2, index_arr, index_arr - grid_len)


def wave_tables(grid_len, row_freq, col_freq, sign_val, factor):
    phase = row_freq[:, None] * col_freq[None, :] % grid_len
    angle = 2.0 * jnp.pi / grid_len * phase.astype(jnp.float32)
    return (jnp.cos(angle) * factor, jnp.sin(angle) * (sign_val * factor))


def block_table(cos_table, sin_table):
    upper = jnp.concatenate([cos_table, sin_table], axis=1)
    lower = jnp.concatenate([-sin_table, cos_table], axis=1)
    return jnp.concatenate([upper, lower], axis=0)


def quarter_turn(grid_vals):
    half_len = grid_vals.shape[-1] // 2
    return jnp.concatenate([-grid_vals[..., half_len:], grid_vals[..., :half_len]], axis=-1)


def mix_dim(grid_vals, cos_table, sin_table, pattern):
    direct = jnp.einsum(pattern, cos_table, grid_vals, precision=top_precision)
    turned = jnp.einsum(pattern, sin_table, quarter_turn(grid_vals), precision=top_precision)
    return direct + turned


def mix_last(grid_vals, table_full):
    row_width = grid_vals.shape[-1]
    product = jnp.dot(
        grid_vals.reshape(-1, row_width),
        table_full,
        precision=top_precision,
        preferred_element_type=jnp.float32,
    )
    return product.reshape(grid_vals.shape)


def band_dot(left_vec, right_vec, weight):
    return jnp.sum(left_vec * right_vec * weight, axis=(0, 2))


def per_band(values):
    return values[None, :, None]


def pair_products(left_vec, right_vec):

    def contract(first_part, second_part):
        return jnp.einsum("bg,cg->bc", first_part, second_part, precision=top_precision)

    real_part = contract(left_vec[0], right_vec[0]) + contract(left_vec[1], right_vec[1])
    imag_part = contract(left_vec[0], right_vec[1]) - contract(left_vec[1], right_vec[0])
    return jnp.stack([real_part, imag_part])


def precondition(residual, kinetic, kin_level):
    x_ratio = kinetic[None, :] / (1.5 * kin_level[:, None] + 1.0)
    numer_poly = 27.0 + x_ratio * (18.0 + x_ratio * (12.0 + 8.0 * x_ratio))
    square = x_ratio * x_ratio
    return residual * (numer_poly / (numer_poly + 16.0 * square * square))[None]


def coupling_matrix(proj_atom, proj_chan, strengths):
    atom_count = strengths.shape[0]
    chan_count = strengths.shape[1]
    symmetric = 0.5 * (strengths + jnp.swapaxes(strengths, 1, 2))
    atom_hot = (proj_atom[:, None] == jnp.arange(atom_count, dtype=jnp.int32)[None, :]).astype(
        jnp.float32
    )
    chan_hot = (proj_chan[:, None] == jnp.arange(chan_count, dtype=jnp.int32)[None, :]).astype(
        jnp.float32
    )
    rows_d = jnp.einsum("pa,pc,acd->pd", atom_hot, chan_hot, symmetric, precision=top_precision)
    same_atom = jnp.dot(
        atom_hot, atom_hot.T, precision=top_precision, preferred_element_type=jnp.float32
    )
    return same_atom * jnp.dot(
        rows_d, chan_hot.T, precision=top_precision, preferred_element_type=jnp.float32
    )


def combine(term_list):
    merged = {}
    for scalar, coef_map in term_list:
        for index_one, coef_a in coef_map.items():
            merged[index_one] = merged.get(index_one, 0.0) + scalar * coef_a
    return merged


def gram_form(gram_table, left_map, right_map, use_kin):
    running = 0.0
    for index_one, coef_a in left_map.items():
        for index_two, coef_b in right_map.items():
            running = running + coef_a * coef_b * gram_table[use_kin, index_one, index_two]
    return running


def new_pairs(first_new, last_new, kinds):
    pair_list = []
    for use_kin in kinds:
        for index_two in range(first_new, last_new):
            for index_one in range(index_two + 1):
                pair_list.append((index_one, index_two, use_kin))
    return pair_list


def body(coeffs, cell_map, potential, projectors, strengths, proj_atom, proj_chan):
    ga_count = lax.axis_size("ga")
    grid_len = potential.shape[0]
    planes = grid_len // ga_count
    band_local = coeffs.shape[1]
    total_pw = coeffs.shape[2] * ga_count
    device = lax.axis_index("ga")
    plane_num = cell_map // (grid_len * grid_len)
    y_index = cell_map // grid_len % grid_len
    z_index = cell_map % grid_len
    freq_x = signed_freq(device + ga_count * plane_num, grid_len)
    freq_y = signed_freq(y_index, grid_len)
    freq_z = signed_freq(z_index, grid_len)
    kinetic = kin_unit * (freq_x * freq_x + freq_y * freq_y + freq_z * freq_z).astype(jnp.float32)
    kin_weight = kinetic[None, None, :]
    slot_re = (plane_num * grid_len + y_index) * (2 * grid_len) + z_index
    slot_im = slot_re + grid_len
    cell_count = planes * grid_len * 2 * grid_len
    natural = jnp.arange(grid_len, dtype=jnp.int32)
    cyclic = natural % planes * ga_count + natural // planes
    cos_fwd, sin_fwd = wave_tables(grid_len, natural, natural, 1.0, 1.0)
    cos_back, sin_back = wave_tables(grid_len, natural, natural, -1.0, 1.0 / grid_len)
    z_forward = block_table(cos_fwd, sin_fwd)
    z_backward = block_table(cos_back, sin_back)
    xcos_fwd, xsin_fwd = wave_tables(grid_len, natural, cyclic, 1.0, 1.0)
    xcos_back, xsin_back = wave_tables(grid_len, cyclic, natural, -1.0, 1.0 / grid_len)
    doubled = jnp.concatenate([potential, potential], axis=-1)
    coupling = coupling_matrix(proj_atom, proj_chan, strengths)

    def real_space(grid_vals):
        grid_vals = mix_dim(grid_vals, xcos_fwd, xsin_fwd, "kj,bjyw->bkyw")
        grid_vals = grid_vals * doubled[None]
        grid_vals = mix_dim(grid_vals, xcos_back, xsin_back, "jk,bkyw->bjyw")
        return lax.all_to_all(grid_vals, "ga", split_axis=1, concat_axis=2, tiled=True)

    def local_part(vectors):
        item_count = vectors.shape[1]
        flat_grid = jnp.zeros((item_count, cell_count), jnp.float32)
        flat_grid = flat_grid.at[:, slot_re].set(vectors[0]).at[:, slot_im].set(vectors[1])
        grid_vals = mix_last(
            flat_grid.reshape(item_count, planes, grid_len, 2 * grid_len), z_forward
        )
        grid_vals = mix_dim(grid_vals, cos_fwd, sin_fwd, "ky,bpyw->bpkw")
        grid_vals = real_space(
            lax.all_to_all(grid_vals, "ga", split_axis=2, concat_axis=1, tiled=True)
        )
        grid_vals = mix_dim(grid_vals, cos_back, sin_back, "ky,bpyw->bpkw")
        flat_grid = mix_last(grid_vals, z_backward).reshape(item_count, cell_count)
        return jnp.stack([flat_grid[:, slot_re], flat_grid[:, slot_im]])

    def contract(first_part, second_part):
        return jnp.einsum("pg,bg->pb", first_part, second_part, precision=top_precision)

    def spread(weights, proj_table):
        return jnp.einsum("pb,pg->bg", weights, proj_table, precision=top_precision)

    def projected_part(vectors):
        proj_re = contract(projectors[0], vectors[0]) + contract(projectors[1], vectors[1])
        proj_im = contract(projectors[0], vectors[1]) - contract(projectors[1], vectors[0])
        proj_re, proj_im = lax.psum((proj_re, proj_im), "ga")
        mixed_re = jnp.dot(
            coupling,
            proj_re / total_pw,
            precision=top_precision,
            preferred_element_type=jnp.float32,
        )
        mixed_im = jnp.dot(
            coupling,
            proj_im / total_pw,
            precision=top_precision,
            preferred_element_type=jnp.float32,
        )
        out_re = spread(mixed_re, projectors[0]) - spread(mixed_im, projectors[1])
        out_im = spread(mixed_re, projectors[1]) + spread(mixed_im, projectors[0])
        return jnp.stack([out_re, out_im])

    def apply_h(vectors):
        return kin_weight * vectors + local_part(vectors) + projected_part(vectors)

    def gram_sums(basis, pair_list):
        stacked = []
        for index_one, index_two, use_kin in pair_list:
            stacked.append(
                band_dot(basis[index_one], basis[index_two], kin_weight if use_kin else 1.0)
            )
        summed = lax.psum(jnp.stack(stacked), "ga") / total_pw
        found = {}
        for slot_num, entry in enumerate(pair_list):
            index_one, index_two, use_kin = entry
            found[use_kin, index_one, index_two] = summed[slot_num]
            found[use_kin, index_two, index_one] = summed[slot_num]
        return found

    def realize(coef_map, basis):
        running = jnp.zeros_like(basis[0])
        for index_one, coef_a in coef_map.items():
            running = (
                running
                + per_band(jnp.zeros((band_local,), jnp.float32) + coef_a) * basis[index_one]
            )
        return running

    h_zero = apply_h(coeffs)
    basis = [coeffs, h_zero]
    gram_table = gram_sums(basis, new_pairs(0, 2, (False, True)))
    psi_map = {0: 1.0}
    ham_map = {1: 1.0}
    eps_zero = gram_form(gram_table, psi_map, ham_map, False) / (
        gram_form(gram_table, psi_map, psi_map, False) + small_eps
    )
    r_map = combine([(1.0, ham_map), (-eps_zero, psi_map)])
    level_zero = gram_form(gram_table, r_map, r_map, True) / (
        gram_form(gram_table, r_map, r_map, False) + small_eps
    )
    p_zero = precondition(realize(r_map, basis), kinetic, level_zero)
    g_zero = apply_h(p_zero)
    basis = [coeffs, h_zero, p_zero, g_zero]
    gram_table.update(gram_sums(basis, new_pairs(2, 4, (False, True))))
    q_map = combine([(1.0, {3: 1.0}), (-eps_zero, {2: 1.0})])
    lam_zero = -gram_form(gram_table, r_map, q_map, False) / (
        gram_form(gram_table, q_map, q_map, False) + small_eps
    )
    psi_one_map = combine([(1.0, psi_map), (lam_zero, {2: 1.0})])
    h_one_map = combine([(1.0, ham_map), (lam_zero, {3: 1.0})])
    eps_one = gram_form(gram_table, psi_one_map, h_one_map, False) / (
        gram_form(gram_table, psi_one_map, psi_one_map, False) + small_eps
    )
    r_one_map = combine([(1.0, h_one_map), (-eps_one, psi_one_map)])
    change_map = combine([(1.0, r_map), (-1.0, r_one_map)])
    weight_one = gram_form(gram_table, r_map, change_map, False) / (
        gram_form(gram_table, change_map, change_map, False) + small_eps
    )
    step_mid = weight_one * lam_zero
    psi_mid_map = combine([(1.0, psi_map), (step_mid, {2: 1.0})])
    h_mid_map = combine([(1.0, ham_map), (step_mid, {3: 1.0})])
    r_mid_map = combine([(1.0, r_map), (-weight_one, change_map)])
    eps_mid = gram_form(gram_table, psi_mid_map, h_mid_map, False) / (
        gram_form(gram_table, psi_mid_map, psi_mid_map, False) + small_eps
    )
    level_mid = gram_form(gram_table, r_mid_map, r_mid_map, True) / (
        gram_form(gram_table, r_mid_map, r_mid_map, False) + small_eps
    )
    p_one = precondition(realize(r_mid_map, basis), kinetic, level_mid)
    g_one = apply_h(p_one)
    basis = [coeffs, h_zero, p_zero, g_zero, p_one, g_one]
    gram_table.update(gram_sums(basis, new_pairs(4, 6, (False,))))
    q_one_map = combine([(1.0, {5: 1.0}), (-eps_mid, {4: 1.0})])
    lam_one = -gram_form(gram_table, r_mid_map, q_one_map, False) / (
        gram_form(gram_table, q_one_map, q_one_map, False) + small_eps
    )
    new_map = combine([(1.0, psi_mid_map), (lam_one, {4: 1.0})])
    ham_new_map = combine([(1.0, h_mid_map), (lam_one, {5: 1.0})])
    norm_new = gram_form(gram_table, new_map, new_map, False) + small_eps
    energy = gram_form(gram_table, new_map, ham_new_map, False) / norm_new
    resid_map = combine([(1.0, ham_new_map), (-energy, new_map)])
    residual_norm = gram_form(gram_table, resid_map, resid_map, False) / norm_new
    new_bands = realize(new_map, basis)
    new_ham = realize(ham_new_map, basis)
    blank_rows = jnp.zeros((2, band_local, band_local * lax.axis_size("band")), jnp.float32)
    first_row = jnp.int32(0)
    over_rows = blank_rows
    ham_rows = blank_rows
    piece_bands = lax.all_gather(new_bands, "band", axis=1, tiled=True)
    piece_ham = lax.all_gather(new_ham, "band", axis=1, tiled=True)
    over_rows = lax.dynamic_update_slice_in_dim(
        over_rows, pair_products(new_bands, piece_bands), first_row, 2
    )
    ham_rows = lax.dynamic_update_slice_in_dim(
        ham_rows, pair_products(new_bands, piece_ham), first_row, 2
    )
    over_rows, ham_rows = (over_rows, ham_rows)
    over_rows, ham_rows = lax.psum((over_rows, ham_rows), "ga")
    correlation = over_rows / total_pw
    subspace = ham_rows / total_pw
    return (new_bands, energy, residual_norm, correlation, subspace)


def solution(mesh):
    placed = (
        P(None, "band", "ga"),
        P("ga"),
        P(None, "ga", None),
        P(None, None, "ga"),
        P(),
        P(),
        P(),
    )
    return jax.shard_map(
        body,
        mesh=mesh,
        in_specs=placed,
        out_specs=(
            P(None, "band", "ga"),
            P("band"),
            P("band"),
            P(None, "band", None),
            P(None, "band", None),
        ),
        check_vma=False,
    )
```

profile of v0, /device:TPU:0, one launch (start us, length us, event | category | flops | bytes accessed | tf_op | source)
XLA Modules:
  0.0 576.9 jit_solution(5087216117158828302)
XLA Ops:
  2.7 9.2 %scatter_custom_fusion = f32[221184]{0:T(1024)S(1)} fusion(s32[2304]{0:T(1024)S(1)} %compare_select_fusion.1, f32[2304]{0:T(1024)S(1)} %get-tuple-element.59, f32[]{:T(128)} %constant.112.clone.1), kind=kCustom, calls=%fused_computation.173 | custom fusion | bytes 884740 | tf_op jit(solution)/shard_map/scatter | solution.py:156
  11.9 9.4 %scatter_fusion = f32[221184]{0:T(1024)S(1)} fusion(f32[221184]{0:T(1024)S(1)} %scatter_custom_fusion, s32[2304]{0:T(1024)S(1)} %get-tuple-element.71, f32[2304]{0:T(1024)S(1)} %get-tuple-element.58), kind=kCustom, calls=%fused_computation.7 | custom fusion | bytes 36864 | tf_op jit(solution)/shard_map/scatter | solution.py:156
  22.7 2.4 fusion.159
  25.4 2.7 fusion.8
  28.1 2.1 copy.144
  30.3 5.3 all-to-all-start
  38.7 20.2 %all-reduce.3 = (f32[64,1]{0,1:T(1,128)S(1)}, f32[64,1]{0,1:T(1,128)S(1)}) all-reduce(f32[64,1]{0,1:T(1,128)S(1)} %fusion.53, f32[64,1]{0,1:T(1,128)S(1)} %fusion.51), channel_id=1, replica_groups=mesh['band'=4,'ga'=8] {'ga'}, use_global_device_ids=true, to_apply=%region_3.4 | all-reduce | flops 128 | bytes 1024 | tf_op jit(solution)/shard_map/psum | solution.py:177
  65.3 1.9 copy.148
  68.4 3.6 fusion.436
  74.2 2.0 copy.218
  76.2 2.4 fusion.150
  82.8 2.5 copy.153
  85.3 3.7 all-to-all-start.1
  90.7 15.1 %all-to-all-done.1 = f32[1,96,12,192]{3,0,2,1:T(1,128)S(1)} async-done(((f32[1,96,12,192]{3,0,2,1:T(1,128)}), f32[1,96,12,192]{3,0,2,1:T(1,128)S(1)}, u32[]{:S(2)}, u32[]{:S(2)}) %all-to-all-start.1) | async-done | bytes 884768 | tf_op jit(solution)/shard_map/all_to_all | solution.py:151
  108.2 2.4 fusion.435
  111.9 2.7 fusion.135
  117.9 12.3 %gather_fusion = f32[2304]{0:T(1024)S(1)} fusion(f32[221184]{0:T(1024)S(1)} %reshape.529, s32[3072]{0:T(1024)S(1)} %pad_clamp_fusion.1), kind=kCustom, calls=%fused_computation | custom fusion | bytes 27648 | tf_op jit(solution)/shard_map/gather | solution.py:166
  130.3 12.3 %gather_fusion.1 = f32[2304]{0:T(1024)S(1)} fusion(f32[221184]{0:T(1024)S(1)} %reshape.529, s32[3072]{0:T(1024)S(1)} %pad_clamp_fusion), kind=kCustom, calls=%fused_computation.1 | custom fusion | bytes 27648 | tf_op jit(solution)/shard_map/gather | solution.py:166
  143.5 4.0 stack.186
  147.5 11.8 %psum.79 = f32[6,1]{0,1:T(1,128)S(1)} all-reduce(f32[6,1]{0,1:T(1,128)S(1)} %stack.186), channel_id=1, replica_groups=mesh['band'=4,'ga'=8] {'ga'}, use_global_device_ids=true, to_apply=%region_10.11 | all-reduce | flops 6 | bytes 48 | tf_op jit(solution)/shard_map/psum | solution.py:203
  165.2 9.4 %scatter_custom_fusion.2 = f32[221184]{0:T(1024)S(1)} fusion(s32[2304]{0:T(1024)} %copy-done.57, f32[2304]{0:T(1024)S(1)} %get-tuple-element.56, f32[]{:T(128)} %constant.112.clone.1), kind=kCustom, calls=%fused_computation.171 | custom fusion | bytes 885248 | tf_op jit(solution)/shard_map/scatter | solution.py:156
  174.6 9.5 %scatter_fusion.1 = f32[221184]{0:T(1024)S(1)} fusion(f32[221184]{0:T(1024)S(1)} %scatter_custom_fusion.2, s32[2304]{0:T(1024)S(1)} %get-tuple-element.71, f32[2304]{0:T(1024)S(1)} %get-tuple-element.55), kind=kCustom, calls=%fused_computation.9 | custom fusion | bytes 36864 | tf_op jit(solution)/shard_map/scatter | solution.py:156
  186.2 2.4 fusion.157
  188.8 2.7 fusion.5
  191.5 2.1 copy.166
  193.7 3.6 all-to-all-start.2
  199.5 21.5 %all-reduce.2 = (f32[64,1]{0,1:T(1,128)}, f32[64,1]{0,1:T(1,128)}) all-reduce(f32[64,1]{0,1:T(1,128)S(1)} %fusion.49, f32[64,1]{0,1:T(1,128)S(1)} %fusion.47), channel_id=1, replica_groups=mesh['band'=4,'ga'=8] {'ga'}, use_global_device_ids=true, to_apply=%region_16.17 | all-reduce | flops 128 | bytes 1024 | tf_op jit(solution)/shard_map/psum | solution.py:177
  222.8 1.9 copy.170
  225.9 3.8 fusion.148
  229.7 2.4 fusion.434
  234.4 2.0 copy.222
  236.3 2.4 fusion.10
  241.5 2.1 copy.173
  243.6 4.1 all-to-all-start.3
  251.6 12.8 %all-to-all-done.3 = f32[1,96,12,192]{3,0,2,1:T(1,128)S(1)} async-done(((f32[1,96,12,192]{3,0,2,1:T(1,128)}), f32[1,96,12,192]{3,0,2,1:T(1,128)S(1)}, u32[]{:S(2)}, u32[]{:S(2)}) %all-to-all-start.3) | async-done | bytes 884768 | tf_op jit(solution)/shard_map/all_to_all | solution.py:151
  269.8 1.6 fusion.433
  271.5 1.6 convolution_add_fusion.4
  275.0 12.3 %gather_fusion.2 = f32[2304]{0:T(1024)S(1)} fusion(f32[221184]{0:T(1024)S(1)} %reshape.549, s32[3072]{0:T(1024)S(1)} %copy-done.54), kind=kCustom, calls=%fused_computation.2 | custom fusion | bytes 27648 | tf_op jit(solution)/shard_map/gather | solution.py:166
  287.4 12.3 %gather_fusion.3 = f32[2304]{0:T(1024)S(1)} fusion(f32[221184]{0:T(1024)S(1)} %reshape.549, s32[3072]{0:T(1024)S(1)} %copy-done.51), kind=kCustom, calls=%fused_computation.3 | custom fusion | bytes 27648 | tf_op jit(solution)/shard_map/gather | solution.py:166
  300.7 8.8 %stack.207 = f32[14,1]{0,1:T(1,128)S(1)} concatenate(f32[1,1]{0,1:T(1,128)} %bitcast.65, f32[1,1]{0,1:T(1,128)} %bitcast.66, f32[1,1]{0,1:T(1,128)} %bitcast.67, f32[1,1]{0,1:T(1,128)} %bitcast.105, f32[1,1]{0,1:T(1,128)} %bitcast.106, f32[1,1]{0,1:T(1,128)} %bitcast.107, f32[1,1]{0,1:T(1,128)} %bitcast.108, f32[1,1]{0,1:T(1,128)} %bitcast.109, f32[1,1]{0,1:T(1,128)} %bitcast.110, ...), dimensions={0} | concatenate | bytes 112 | tf_op jit(solution)/shard_map/stack | solution.py:203
  310.0 11.8 %psum.82 = f32[14,1]{0,1:T(1,128)S(1)} all-reduce(f32[14,1]{0,1:T(1,128)S(1)} %stack.207), channel_id=1, replica_groups=mesh['band'=4,'ga'=8] {'ga'}, use_global_device_ids=true, to_apply=%region_29.30 | all-reduce | flops 14 | bytes 112 | tf_op jit(solution)/shard_map/psum | solution.py:203
  353.6 9.4 %scatter_custom_fusion.4 = f32[221184]{0:T(1024)S(1)} fusion(s32[2304]{0:T(1024)} %copy-done.57, f32[2304]{0:T(1024)S(1)} %get-tuple-element.54, f32[]{:T(128)} %constant.112.clone.1), kind=kCustom, calls=%fused_computation.169 | custom fusion | bytes 885248 | tf_op jit(solution)/shard_map/scatter | solution.py:156
  363.0 9.5 %scatter_fusion.2 = f32[221184]{0:T(1024)S(1)} fusion(f32[221184]{0:T(1024)S(1)} %scatter_custom_fusion.4, s32[2304]{0:T(1024)S(1)} %get-tuple-element.71, f32[2304]{0:T(1024)S(1)} %get-tuple-element.53), kind=kCustom, calls=%fused_computation.11 | custom fusion | bytes 36864 | tf_op jit(solution)/shard_map/scatter | solution.py:156
  374.6 2.4 fusion.155
  377.2 2.7 fusion.2
  380.0 2.1 copy.185
  382.1 3.6 all-to-all-start.4
  388.0 20.9 %all-reduce.1 = (f32[64,1]{0,1:T(1,128)S(1)}, f32[64,1]{0,1:T(1,128)S(1)}) all-reduce(f32[64,1]{0,1:T(1,128)S(1)} %fusion.45, f32[64,1]{0,1:T(1,128)S(1)} %fusion.43), channel_id=1, replica_groups=mesh['band'=4,'ga'=8] {'ga'}, use_global_device_ids=true, to_apply=%region_37.38 | all-reduce | flops 128 | bytes 1024 | tf_op jit(solution)/shard_map/psum | solution.py:177
  410.7 1.9 copy.189
  413.7 3.8 fusion.146
  417.5 2.4 fusion.432
  422.2 2.0 copy.226
  424.2 2.4 fusion.11
  429.4 2.1 copy.192
  431.5 3.9 all-to-all-start.5
  443.2 9.0 %all-to-all-done.5 = f32[1,96,12,192]{3,0,2,1:T(1,128)S(1)} async-done(((f32[1,96,12,192]{3,0,2,1:T(1,128)}), f32[1,96,12,192]{3,0,2,1:T(1,128)S(1)}, u32[]{:S(2)}, u32[]{:S(2)}) %all-to-all-start.5) | async-done | bytes 884768 | tf_op jit(solution)/shard_map/all_to_all | solution.py:151
  457.5 1.6 fusion.431
  462.7 12.3 %gather_fusion.4 = f32[2304]{0:T(1024)S(1)} fusion(f32[221184]{0:T(1024)S(1)} %reshape.569, s32[3072]{0:T(1024)S(1)} %copy-done.55), kind=kCustom, calls=%fused_computation.4 | custom fusion | bytes 27648 | tf_op jit(solution)/shard_map/gather | solution.py:166
  475.1 12.3 %gather_fusion.5 = f32[2304]{0:T(1024)S(1)} fusion(f32[221184]{0:T(1024)S(1)} %reshape.569, s32[3072]{0:T(1024)S(1)} %copy-done.52), kind=kCustom, calls=%fused_computation.5 | custom fusion | bytes 27648 | tf_op jit(solution)/shard_map/gather | solution.py:166
  488.3 7.0 %stack.225 = f32[11,1]{0,1:T(1,128)S(1)} concatenate(f32[1,1]{0,1:T(1,128)} %bitcast.136, f32[1,1]{0,1:T(1,128)} %bitcast.137, f32[1,1]{0,1:T(1,128)} %bitcast.138, f32[1,1]{0,1:T(1,128)} %bitcast.139, f32[1,1]{0,1:T(1,128)} %bitcast.140, f32[1,1]{0,1:T(1,128)} %bitcast.178, f32[1,1]{0,1:T(1,128)} %bitcast.179, f32[1,1]{0,1:T(1,128)} %bitcast.180, f32[1,1]{0,1:T(1,128)} %bitcast.181, ...), dimensions={0} | concatenate | bytes 88 | tf_op jit(solution)/shard_map/stack | solution.py:203
  495.9 11.8 %psum.85 = f32[11,1]{0,1:T(1,128)S(1)} all-reduce(f32[11,1]{0,1:T(1,128)S(1)} %stack.225), channel_id=1, replica_groups=mesh['band'=4,'ga'=8] {'ga'}, use_global_device_ids=true, to_apply=%region_45.46 | all-reduce | flops 11 | bytes 88 | tf_op jit(solution)/shard_map/psum | solution.py:203
  525.3 13.4 %all_gather.7 = f32[2,4,2304]{2,0,1:T(2,128)S(1)} all-gather(f32[2,1,2304]{2,0,1:T(2,128)S(1)} %multiply_add_fusion), channel_id=1, replica_groups=mesh['band'=4,'ga'=8] {'band'}, dimensions={1}, use_global_device_ids=true | all-gather | bytes 92160 | tf_op jit(solution)/shard_map/all_gather | solution.py:281
  538.8 13.2 %all_gather.6 = f32[2,4,2304]{2,0,1:T(2,128)S(1)} all-gather(f32[2,1,2304]{2,0,1:T(2,128)S(1)} %multiply_add_fusion.1), channel_id=1, replica_groups=mesh['band'=4,'ga'=8] {'band'}, dimensions={1}, use_global_device_ids=true | all-gather | bytes 92160 | tf_op jit(solution)/shard_map/all_gather | solution.py:280
  554.9 11.8 %all-reduce = (f32[2,1,4]{2,1,0:T(1,128)S(1)}, f32[2,1,4]{2,1,0:T(1,128)S(1)}) all-reduce(f32[2,1,4]{2,1,0:T(1,128)S(1)} %pad_maximum_fusion, f32[2,1,4]{2,1,0:T(1,128)S(1)} %pad_maximum_fusion.1), channel_id=1, replica_groups=mesh['band'=4,'ga'=8] {'ga'}, use_global_device_ids=true, to_apply=%region_46.47 | all-reduce | flops 16 | bytes 128 | tf_op jit(solution)/shard_map/psum | solution.py:289
  (296 shorter events, 84.2 us)
Async XLA Ops:
  0.9 20.7 %copy-start.31 = (f32[96,96]{1,0:T(8,128)}, f32[96,96]{1,0:T(8,128)S(1)}, u32[]{:S(2)}) copy-start(f32[96,96]{1,0:T(8,128)S(1)} %get-tuple-element.134) | copy-start | bytes 110596
  0.9 20.7 %copy-start.34 = (f32[96,96]{1,0:T(8,128)}, f32[96,96]{1,0:T(8,128)S(1)}, u32[]{:S(2)}) copy-start(f32[96,96]{1,0:T(8,128)S(1)} %get-tuple-element.135) | copy-start | bytes 110596
  1.1 20.5 %copy-start.37 = (f32[96,96]{1,0:T(8,128)}, f32[96,96]{1,0:T(8,128)S(1)}, u32[]{:S(2)}) copy-start(f32[96,96]{1,0:T(8,128)S(1)} %fusion.244) | copy-start | bytes 110596
  1.9 19.4 %copy-start.57 = (s32[2304]{0:T(1024)}, s32[2304]{0:T(1024)S(1)}, u32[]{:S(2)}) copy-start(s32[2304]{0:T(1024)S(1)} %compare_select_fusion.1) | copy-start | bytes 27652
  30.3 5.3 copy-start
  30.3 5.3 copy-start.16
  30.3 33.2 %all-to-all-start = ((f32[1,12,96,192]{3,0,1,2:T(1,128)}), f32[1,12,96,192]{3,0,1,2:T(1,128)S(1)}, u32[]{:S(2)}, u32[]{:S(2)}) async-start(f32[1,12,96,192]{3,0,1,2:T(1,128)} %copy.144), calls=%async_computation | async-start | bytes 2359296 | tf_op jit(solution)/shard_map/all_to_all | solution.py:162
  38.7 23.1 %copy-start.13 = (f32[64,64]{1,0:T(8,128)}, f32[64,64]{1,0:T(8,128)S(1)}, u32[]{:S(2)}) copy-start(f32[64,64]{1,0:T(8,128)S(1)} %convolution_multiply_fusion) | copy-start | bytes 49156
  60.3 18.3 %copy-start.1 = (f32[96,12,96]{0,2,1:T(8,128)}, f32[96,12,96]{0,2,1:T(8,128)S(1)}, u32[]{:S(2)}) copy-start(f32[96,12,96]{0,2,1:T(8,128)S(1)} %copy.151) | copy-start | bytes 1327108
  73.0 3.2 copy-start.7
  76.2 2.5 copy-start.8
  85.3 3.7 copy-start.65
  85.3 4.1 copy-start.59
  85.3 4.8 copy-start.58
  85.3 5.3 copy-start.45
  85.3 20.4 %all-to-all-start.1 = ((f32[1,96,12,192]{3,0,2,1:T(1,128)}), f32[1,96,12,192]{3,0,2,1:T(1,128)S(1)}, u32[]{:S(2)}, u32[]{:S(2)}) async-start(f32[1,96,12,192]{3,0,2,1:T(1,128)} %copy.153), calls=%async_computation.1 | async-start | bytes 2359296 | tf_op jit(solution)/shard_map/all_to_all | solution.py:151
  90.1 27.8 %copy-start.53 = (s32[3072]{0:T(1024)}, s32[3072]{0:T(1024)S(1)}, u32[]{:S(2)}) copy-start(s32[3072]{0:T(1024)S(1)} %pad_clamp_fusion.1) | copy-start | bytes 36868
  90.1 40.2 %copy-start.50 = (s32[3072]{0:T(1024)}, s32[3072]{0:T(1024)S(1)}, u32[]{:S(2)}) copy-start(s32[3072]{0:T(1024)S(1)} %pad_clamp_fusion) | copy-start | bytes 36868
  90.3 25.8 %copy-start.22 = (f32[96,96]{1,0:T(8,128)}, f32[96,96]{1,0:T(8,128)S(1)}, u32[]{:S(2)}) copy-start(f32[96,96]{1,0:T(8,128)S(1)} %fusion.245) | copy-start | bytes 110596
  90.6 25.5 %copy-start.25 = (f32[96,96]{1,0:T(8,128)}, f32[96,96]{1,0:T(8,128)S(1)}, u32[]{:S(2)}) copy-start(f32[96,96]{1,0:T(8,128)S(1)} %get-tuple-element.136) | copy-start | bytes 110596
  90.6 25.5 %copy-start.28 = (f32[96,96]{1,0:T(8,128)}, f32[96,96]{1,0:T(8,128)S(1)}, u32[]{:S(2)}) copy-start(f32[96,96]{1,0:T(8,128)S(1)} %get-tuple-element.137) | copy-start | bytes 110596
  90.7 52.0 %copy-start.47 = (f32[2304]{0:T(1024)}, f32[2304]{0:T(1024)S(1)}, u32[]{:S(2)}) copy-start(f32[2304]{0:T(1024)S(1)} %fusion.272) | copy-start | bytes 27652
  108.2 2.5 copy-start.4
  111.9 2.7 copy-start.9
  130.3 12.4 %copy-start.17 = (f32[2,1,2304]{2,1,0:T(1,128)S(1)}, f32[2,1,2304]{2,1,0:T(1,128)}, u32[]{:S(2)}) copy-start(f32[2,1,2304]{2,1,0:T(1,128)} %param.7) | copy-start | bytes 55300
  130.3 12.4 %copy-start.62 = (f32[1,1,2304]{2,0,1:T(1,128)S(1)}, f32[1,1,2304]{2,0,1:T(1,128)}, u32[]{:S(2)}) copy-start(f32[1,1,2304]{2,0,1:T(1,128)} %stack.178) | copy-start | bytes 27652
  130.3 12.4 %copy-start.63 = (f32[1,1,2304]{2,0,1:T(1,128)S(1)}, f32[1,1,2304]{2,0,1:T(1,128)}, u32[]{:S(2)}) copy-start(f32[1,1,2304]{2,0,1:T(1,128)} %stack.179) | copy-start | bytes 27652
  143.5 21.8 %copy-start.40 = (f32[2,1,2304]{2,0,1:T(2,128)}, f32[2,1,2304]{2,0,1:T(2,128)S(1)}, u32[]{:S(2)}) copy-start(f32[2,1,2304]{2,0,1:T(2,128)S(1)} %get-tuple-element.70) | copy-start | bytes 55300
  165.1 33.8 %copy-start.10 = (f32[2,1,2304]{2,0,1:T(2,128)}, f32[2,1,2304]{2,0,1:T(2,128)S(1)}, u32[]{:S(2)}) copy-start(f32[2,1,2304]{2,0,1:T(2,128)S(1)} %add_multiply_fusion.1) | copy-start | bytes 55300
  193.7 27.3 %all-to-all-start.2 = ((f32[1,12,96,192]{3,0,1,2:T(1,128)}), f32[1,12,96,192]{3,0,1,2:T(1,128)S(1)}, u32[]{:S(2)}, u32[]{:S(2)}) async-start(f32[1,12,96,192]{3,0,1,2:T(1,128)} %copy.166), calls=%async_computation.2 | async-start | bytes 2359296 | tf_op jit(solution)/shard_map/all_to_all | solution.py:162
  225.9 3.8 copy-start.5
  233.2 3.2 copy-start.2
  243.6 4.1 copy-start.14
  243.6 4.1 copy-start.69
  243.6 5.4 copy-start.68
  243.6 20.8 %all-to-all-start.3 = ((f32[1,96,12,192]{3,0,2,1:T(1,128)}), f32[1,96,12,192]{3,0,2,1:T(1,128)S(1)}, u32[]{:S(2)}, u32[]{:S(2)}) async-start(f32[1,96,12,192]{3,0,2,1:T(1,128)} %copy.173), calls=%async_computation.3 | async-start | bytes 2359296 | tf_op jit(solution)/shard_map/all_to_all | solution.py:151
  271.4 1.6 copy-start.23
  271.5 1.6 copy-start.26
  271.5 1.6 copy-start.29
  275.0 12.3 %copy-start.51 = (s32[3072]{0:T(1024)S(1)}, s32[3072]{0:T(1024)}, u32[]{:S(2)}) copy-start(s32[3072]{0:T(1024)} %copy-done.50) | copy-start | bytes 36868
  287.3 12.4 %copy-start.11 = (f32[2,1,2304]{2,0,1:T(2,128)S(1)}, f32[2,1,2304]{2,0,1:T(2,128)}, u32[]{:S(2)}) copy-start(f32[2,1,2304]{2,0,1:T(2,128)} %copy-done.10) | copy-start | bytes 55300
  287.4 12.4 %copy-start.18 = (f32[2,1,2304]{2,1,0:T(1,128)S(1)}, f32[2,1,2304]{2,1,0:T(1,128)}, u32[]{:S(2)}) copy-start(f32[2,1,2304]{2,1,0:T(1,128)} %param.7) | copy-start | bytes 55300
  287.4 12.4 %copy-start.41 = (f32[2,1,2304]{2,0,1:T(2,128)S(1)}, f32[2,1,2304]{2,0,1:T(2,128)}, u32[]{:S(2)}) copy-start(f32[2,1,2304]{2,0,1:T(2,128)} %copy-done.40) | copy-start | bytes 55300
  287.4 12.4 %copy-start.48 = (f32[2304]{0:T(1024)S(1)}, f32[2304]{0:T(1024)}, u32[]{:S(2)}) copy-start(f32[2304]{0:T(1024)} %copy-done.47) | copy-start | bytes 27652
  287.4 12.4 %copy-start.60 = (f32[1,1,2304]{2,0,1:T(1,128)S(1)}, f32[1,1,2304]{2,0,1:T(1,128)}, u32[]{:S(2)}) copy-start(f32[1,1,2304]{2,0,1:T(1,128)} %stack.193) | copy-start | bytes 27652
  287.4 12.4 %copy-start.61 = (f32[1,1,2304]{2,0,1:T(1,128)S(1)}, f32[1,1,2304]{2,0,1:T(1,128)}, u32[]{:S(2)}) copy-start(f32[1,1,2304]{2,0,1:T(1,128)} %stack.194) | copy-start | bytes 27652
  287.4 66.1 %copy-start.46 = (s32[2304]{0:T(1024)S(1)}, s32[2304]{0:T(1024)}, u32[]{:S(2)}) copy-start(s32[2304]{0:T(1024)} %param.8) | copy-start | bytes 27652
  300.7 62.3 %copy-start.43 = (f32[2,1,2304]{2,0,1:T(2,128)}, f32[2,1,2304]{2,0,1:T(2,128)S(1)}, u32[]{:S(2)}) copy-start(f32[2,1,2304]{2,0,1:T(2,128)S(1)} %get-tuple-element.69) | copy-start | bytes 55300
  353.6 33.8 %copy-start.20 = (f32[2,1,2304]{2,0,1:T(2,128)}, f32[2,1,2304]{2,0,1:T(2,128)S(1)}, u32[]{:S(2)}) copy-start(f32[2,1,2304]{2,0,1:T(2,128)S(1)} %add_multiply_fusion) | copy-start | bytes 55300
  382.1 26.8 %all-to-all-start.4 = ((f32[1,12,96,192]{3,0,1,2:T(1,128)}), f32[1,12,96,192]{3,0,1,2:T(1,128)S(1)}, u32[]{:S(2)}, u32[]{:S(2)}) async-start(f32[1,12,96,192]{3,0,1,2:T(1,128)} %copy.185), calls=%async_computation.4 | async-start | bytes 2359296 | tf_op jit(solution)/shard_map/all_to_all | solution.py:162
  413.7 3.8 copy-start.6
  421.0 3.2 copy-start.3
  431.5 4.0 copy-start.15
  431.5 20.7 %all-to-all-start.5 = ((f32[1,96,12,192]{3,0,2,1:T(1,128)}), f32[1,96,12,192]{3,0,2,1:T(1,128)S(1)}, u32[]{:S(2)}, u32[]{:S(2)}) async-start(f32[1,96,12,192]{3,0,2,1:T(1,128)} %copy.192), calls=%async_computation.5 | async-start | bytes 2359296 | tf_op jit(solution)/shard_map/all_to_all | solution.py:151
  459.1 1.6 copy-start.24
  459.2 1.6 copy-start.27
  459.2 1.6 copy-start.30
  462.7 12.3 %copy-start.52 = (s32[3072]{0:T(1024)S(1)}, s32[3072]{0:T(1024)}, u32[]{:S(2)}) copy-start(s32[3072]{0:T(1024)} %copy-done.50) | copy-start | bytes 36868
  475.0 12.4 %copy-start.12 = (f32[2,1,2304]{2,0,1:T(2,128)S(1)}, f32[2,1,2304]{2,0,1:T(2,128)}, u32[]{:S(2)}) copy-start(f32[2,1,2304]{2,0,1:T(2,128)} %copy-done.10) | copy-start | bytes 55300
  475.0 12.4 %copy-start.19 = (f32[2,1,2304]{2,1,0:T(1,128)S(1)}, f32[2,1,2304]{2,1,0:T(1,128)}, u32[]{:S(2)}) copy-start(f32[2,1,2304]{2,1,0:T(1,128)} %param.7) | copy-start | bytes 55300
  475.1 12.4 %copy-start.21 = (f32[2,1,2304]{2,0,1:T(2,128)S(1)}, f32[2,1,2304]{2,0,1:T(2,128)}, u32[]{:S(2)}) copy-start(f32[2,1,2304]{2,0,1:T(2,128)} %copy-done.20) | copy-start | bytes 55300
  475.1 12.4 %copy-start.42 = (f32[2,1,2304]{2,0,1:T(2,128)S(1)}, f32[2,1,2304]{2,0,1:T(2,128)}, u32[]{:S(2)}) copy-start(f32[2,1,2304]{2,0,1:T(2,128)} %copy-done.40) | copy-start | bytes 55300
  475.1 12.4 %copy-start.44 = (f32[2,1,2304]{2,0,1:T(2,128)S(1)}, f32[2,1,2304]{2,0,1:T(2,128)}, u32[]{:S(2)}) copy-start(f32[2,1,2304]{2,0,1:T(2,128)} %copy-done.43) | copy-start | bytes 55300
  475.1 12.4 %copy-start.49 = (f32[2304]{0:T(1024)S(1)}, f32[2304]{0:T(1024)}, u32[]{:S(2)}) copy-start(f32[2304]{0:T(1024)} %copy-done.47) | copy-start | bytes 27652
  (12 other events, 10.8 us)
where the time goes:
time: 588 us; the launch traced here: 577 us
  local copies, waits for them, and re-layouts  225 us (38%)
  blocking collectives  136 us (23%)
  matrix products  72.4 us (12%)
  between operations  72.1 us (12%)
  waiting for transfers between devices  36.9 us (6%)
  starting transfers between devices  24.2 us (4%)
  other arithmetic  10.1 us (2%)
    gather x6, local copies, waits for them, and re-layouts, local_part(): return jnp.stack([flat_grid[:, slot_re], flat_grid[:, slot_im]])  73.9 us
    psum x3, blocking collectives, projected_part(): proj_re, proj_im = lax.psum((proj_re, proj_im), 'ga')  62.5 us
    scatter x6, local copies, waits for them, and re-layouts, local_part(): flat_grid.at[:, slot_re].set(vectors[0]).at[:, slot_im].set(vectors[1])  56.4 us
    all_to_all x3, waiting for transfers between devices, real_space(): lax.all_to_all(grid_vals, 'ga', split_axis=1, concat_axis=2, tiled=True)  36.9 us
    psum x3, blocking collectives, gram_sums(): summed = lax.psum(jnp.stack(stacked), 'ga') / total_pw  35.4 us
    dot_general x12, matrix products, mix_dim(): direct = jnp.einsum(pattern, cos_table, grid_vals, precision=top_precision)  26.6 us
    dot_general x12, matrix products, mix_dim(): jnp.einsum(pattern, sin_table, quarter_turn(grid_vals), precision=top_pre...  23 us
    another operation x3, local copies, waits for them, and re-layouts, gram_sums(): summed = lax.psum(jnp.stack(stacked), 'ga') / total_pw  19.8 us
  transfers between devices with their start and end apart: 6, of which 3 were waited for; matrix products, arithmetic and copies ran while one was open for 3% of the time, Pallas kernels for 0%

commit v1 on v0

--- a/solution.py
+++ b/solution.py
@@ -1,6 +1,11 @@
+import functools
+
 import jax
 import jax.numpy as jnp
+import numpy as np
 from jax import lax
+from jax.experimental import pallas as pl
+from jax.experimental.pallas import tpu as pltpu
 from jax.sharding import PartitionSpec as P
 
 top_precision = lax.Precision.HIGHEST
@@ -115,7 +120,7 @@
     return pair_list
 
 
-def body(coeffs, cell_map, potential, projectors, strengths, proj_atom, proj_chan):
+def plain_body(coeffs, cell_map, potential, projectors, strengths, proj_atom, proj_chan):
     ga_count = lax.axis_size("ga")
     grid_len = potential.shape[0]
     planes = grid_len // ga_count
@@ -292,6 +297,444 @@
     return (new_bands, energy, residual_norm, correlation, subspace)
 
 
+QUAD = 4
+TRIPLE = 3
+MESH = pl.DeviceIdType.MESH
+
+
+def split_const(values):
+    high = np.asarray(values, np.float32).astype(jnp.bfloat16)
+    low = (values - high.astype(np.float64)).astype(np.float32).astype(jnp.bfloat16)
+    return np.stack([high, low])
+
+
+def const_tables(grid_len, group):
+    planes = grid_len // group
+    chunks = planes // QUAD
+    unit = 2.0 * np.pi / grid_len
+    quarter = grid_len / 4.0
+    chunk = np.arange(chunks)[:, None, None, None]
+    dev = np.arange(group)[None, :, None, None]
+    part = np.arange(2)[None, None, :, None]
+    inner = np.arange(QUAD)[None, None, None, :]
+    y_real = (dev * planes + chunk * QUAD + inner + 0 * part).reshape(-1)
+    part_row = (part + 0 * (dev + chunk + inner)).reshape(-1)
+    freq = np.arange(grid_len)
+    phase = (y_real[:, None] * freq[None, :]) % grid_len
+    tab_a = np.cos(unit * (phase - quarter * part_row[:, None]))
+    tab_b = np.cos(unit * (phase + quarter * (1 - part_row[:, None])))
+    wave = split_const(np.concatenate([tab_a, tab_b], axis=0))
+    four = np.repeat(np.arange(4), grid_len)
+    zed = np.tile(freq, 4)
+    theta = 2.0 * np.pi * ((four[:, None] * four[None, :] % 4) / 4.0
+                           + (zed[:, None] * zed[None, :] % grid_len) / grid_len)
+    fourz = split_const(np.concatenate([np.cos(theta), np.sin(theta)], axis=1))
+    dft = 2.0 * np.pi * np.outer(np.arange(group), np.arange(group)) / group
+    real_mix = np.zeros((group, 2, QUAD, group, 2, QUAD))
+    for row in range(QUAD):
+        real_mix[:, 0, row, :, 0, row] = np.cos(dft)
+        real_mix[:, 1, row, :, 1, row] = np.cos(dft)
+        real_mix[:, 0, row, :, 1, row] = -np.sin(dft)
+        real_mix[:, 1, row, :, 0, row] = np.sin(dft)
+    size = group * 2 * QUAD
+    real_mix = real_mix.reshape(size, size)
+
+    def stacked(mat):
+        high, low = split_const(mat)
+        return np.concatenate([high, high, low], axis=1)
+
+    across = np.stack([stacked(real_mix), stacked(real_mix.T)])
+    b_lane = np.repeat(np.arange(TRIPLE), 4 * grid_len)
+    a_lane = np.tile(np.repeat(np.arange(4), grid_len), TRIPLE)
+    one = 2.0 * np.pi * (a_lane * b_lane) / planes
+    two = unit * np.outer(np.arange(group), TRIPLE * a_lane + b_lane)
+    lane_tw = np.stack([np.cos(one), np.sin(one)]).astype(np.float32)[:, None, :]
+    dev_tw = np.stack([np.cos(two), np.sin(two)]).astype(np.float32)[:, :, None, :]
+    return wave, fourz, across, lane_tw, dev_tw
+
+
+def two_parts(values):
+    high = values.astype(jnp.bfloat16)
+    low = (values - high.astype(jnp.float32)).astype(jnp.bfloat16)
+    return high, low
+
+
+def bdot(left, right):
+    return jnp.dot(left, right, preferred_element_type=jnp.float32)
+
+
+def sweep_kernel(
+    dims,
+    coeffs_ref, kin_ref, ynum_ref, key_row_ref, key_col_ref, pot_ref, proj_ref, coup_ref,
+    wave_ref, fourz_ref, across_ref, lane_ref, dev_ref,
+    new_ref, scal_ref,
+    hot_ref, hot_t_ref, ta_ref, tb_ref,
+    fsend, frecv, bsend, brecv, psend, precv, gsend, grecv, nsend, nrecv, csend, crecv,
+    fs_sem, fr_sem, bs_sem, br_sem, ps_sem, pr_sem, gs_sem, gr_sem, ns_sem, nr_sem, cs_sem, cr_sem,
+):
+    group, bands, chunks, grid_len, total_pw, pw = dims
+    rows = group * 2 * QUAD
+    lanes = TRIPLE * 4 * grid_len
+    quad_lanes = 4 * grid_len
+    me = lax.axis_index("ga")
+    band = lax.axis_index("band")
+
+    barrier = pltpu.get_barrier_semaphore()
+    for off in range(1, group):
+        pl.semaphore_signal(barrier, inc=1, device_id={"ga": lax.rem(me + off, group)}, device_id_type=MESH)
+    for off in range(1, bands):
+        pl.semaphore_signal(barrier, inc=1, device_id={"band": lax.rem(band + off, bands)}, device_id_type=MESH)
+
+    hot_rows = 256
+
+    def build_hot(step, carry):
+        at = pl.multiple_of(step * hot_rows, hot_rows)
+        lane_id = lax.broadcasted_iota(jnp.int32, (hot_rows, lanes), 1)
+        hot_ref[pl.ds(at, hot_rows), :] = (lane_id == key_col_ref[pl.ds(at, hot_rows), :]).astype(jnp.float32).astype(jnp.bfloat16)
+        return carry
+
+    lax.fori_loop(0, pw // hot_rows, build_hot, 0)
+    turn_rows = 128
+
+    def build_turn(step, carry):
+        at = pl.multiple_of(step * turn_rows, turn_rows)
+        row_id = lax.broadcasted_iota(jnp.int32, (turn_rows, pw), 0) + at
+        hot_t_ref[pl.ds(at, turn_rows), :] = (row_id == key_row_ref[...]).astype(jnp.float32).astype(jnp.bfloat16)
+        return carry
+
+    lax.fori_loop(0, lanes // turn_rows, build_turn, 0)
+    y_hot = (lax.broadcasted_iota(jnp.int32, (grid_len, pw), 0) == ynum_ref[...]).astype(jnp.float32).astype(jnp.bfloat16)
+    for part in range(chunks):
+        for table, base in ((ta_ref, 0), (tb_ref, chunks * rows)):
+            at = base + part * rows
+            table[part] = bdot(wave_ref[0, at:at + rows, :], y_hot) + bdot(wave_ref[1, at:at + rows, :], y_hot)
+
+    pl.semaphore_wait(barrier, group + bands - 2)
+
+    kin = kin_ref[...]
+    sign = jnp.where(lax.broadcasted_iota(jnp.int32, (1, 2 * QUAD, 1), 1) < QUAD, -1.0, 1.0).astype(jnp.float32)
+
+    def times_i(values):
+        return pltpu.roll(values, QUAD, 1) * sign
+
+    def lane_split(values):
+        return [values[..., k * quad_lanes:(k + 1) * quad_lanes] for k in range(TRIPLE)]
+
+    def mix_fourz(triple, direction):
+        stacked = jnp.concatenate([t.reshape(rows, quad_lanes) for t in triple], axis=0)
+        high, low = two_parts(stacked)
+        out = bdot(high, fourz_ref[0]) + bdot(low, fourz_ref[0]) + bdot(high, fourz_ref[1])
+        out = out.reshape(TRIPLE * group, 2 * QUAD, 2 * quad_lanes)
+        mixed = out[..., :quad_lanes] + direction * times_i(out[..., quad_lanes:])
+        return [mixed[k * group:(k + 1) * group] for k in range(TRIPLE)]
+
+    def turn_lane(triple, direction):
+        done = [triple[0]]
+        for k in range(1, TRIPLE):
+            at = slice(k * quad_lanes, (k + 1) * quad_lanes)
+            done.append(triple[k] * lane_ref[0, :, at][None] + direction * times_i(triple[k]) * lane_ref[1, :, at][None])
+        return done
+
+    def three(triple, direction):
+        total = triple[1] + triple[2]
+        diff = times_i(triple[1] - triple[2]) * (direction * 0.8660254037844386)
+        base = triple[0] - 0.5 * total
+        return [triple[0] + total, base + diff, base - diff]
+
+    def turn_dev(values, direction):
+        return values * dev_ref[0] + direction * times_i(values) * dev_ref[1]
+
+    def mix_devices(values, which):
+        high, low = two_parts(values.reshape(rows, lanes))
+        return bdot(across_ref[which], jnp.concatenate([high, low, high], axis=0))
+
+    def all_sum(local, send, recv, send_sem, recv_sem, shape_at):
+        send[shape_at] = local
+        recv[shape_at, me] = local
+        for off in range(1, group):
+            pltpu.make_async_remote_copy(
+                src_ref=send.at[shape_at], dst_ref=recv.at[shape_at, me],
+                send_sem=send_sem.at[shape_at, off - 1], recv_sem=recv_sem.at[shape_at, off - 1],
+                device_id={"ga": lax.rem(me + off, group)}, device_id_type=MESH).start()
+
+    def all_sum_end(send, recv, send_sem, recv_sem, shape_at):
+        for off in range(1, group):
+            pltpu.make_async_remote_copy(
+                src_ref=send.at[shape_at], dst_ref=recv.at[shape_at, lax.rem(me + group - off, group)],
+                send_sem=send_sem.at[shape_at, off - 1], recv_sem=recv_sem.at[shape_at, off - 1],
+                device_id={"ga": lax.rem(me + off, group)}, device_id_type=MESH).wait()
+        running = recv[shape_at, 0]
+        for dev in range(1, group):
+            running = running + recv[shape_at, dev]
+        return running
+
+    def piece(turn, part, off, send, recv, send_sem, recv_sem, incoming):
+        peer = lax.rem(me + off, group)
+        source = lax.rem(me + group - off, group) if incoming else me
+        return pltpu.make_async_remote_copy(
+            src_ref=send.at[turn, part, peer], dst_ref=recv.at[turn, part, source],
+            send_sem=send_sem.at[turn, part, off - 1], recv_sem=recv_sem.at[turn, part, off - 1],
+            device_id={"ga": peer}, device_id_type=MESH)
+
+    def apply_h(turn, vector):
+        v_re, v_im = vector[0:1], vector[1:2]
+        fwd = (fsend, frecv, fs_sem, fr_sem)
+        back = (bsend, brecv, bs_sem, br_sem)
+
+        def put(part, carry):
+            high, low = two_parts(ta_ref[part] * v_re + tb_ref[part] * v_im)
+            out = bdot(jnp.concatenate([high, low], axis=0), hot_ref[...])
+            out = (out[:rows] + out[rows:]).reshape(group, 2 * QUAD, lanes)
+            fsend[turn, part] = out
+            frecv[turn, part, me] = fsend[turn, part, me]
+            for off in range(1, group):
+                piece(turn, part, off, *fwd, False).start()
+            return carry
+
+        lax.fori_loop(0, chunks, put, 0)
+        sums = lax.dot_general(vector, proj_ref[...], (((1,), (1,)), ((), ())), precision=top_precision, preferred_element_type=jnp.float32)
+        all_sum(sums, psend, precv, ps_sem, pr_sem, turn)
+
+        def middle(part, carry):
+            for off in range(1, group):
+                piece(turn, part, off, *fwd, True).wait()
+            triple = turn_lane(three(lane_split(frecv[turn, part]), 1.0), 1.0)
+            values = turn_dev(jnp.concatenate(mix_fourz(triple, 1.0), axis=-1), 1.0)
+            values = mix_devices(values, 0) * pot_ref[part]
+            values = mix_devices(values, 1).reshape(group, 2 * QUAD, lanes)
+            triple = mix_fourz(lane_split(turn_dev(values, -1.0)), -1.0)
+            triple = three(turn_lane(triple, -1.0), -1.0)
+            bsend[turn, part] = jnp.concatenate(triple, axis=-1)
+            brecv[turn, part, me] = bsend[turn, part, me]
+            for off in range(1, group):
+                piece(turn, part, off, *back, False).start()
+            return carry
+
+        lax.fori_loop(0, chunks, middle, 0)
+        sums = all_sum_end(psend, precv, ps_sem, pr_sem, turn) * (1.0 / total_pw)
+        direct = jnp.dot(sums, coup_ref[0], precision=top_precision, preferred_element_type=jnp.float32)
+        turned = jnp.dot(sums, coup_ref[1], precision=top_precision, preferred_element_type=jnp.float32)
+        weights = jnp.concatenate([direct[0:1] + turned[1:2], direct[1:2] - turned[0:1]], axis=0)
+        nonlocal_part = jnp.dot(weights, proj_ref[...], precision=top_precision, preferred_element_type=jnp.float32)
+        start = kin * vector + nonlocal_part
+
+        def take(part, carry):
+            run_re, run_im = carry
+            for off in range(1, group):
+                piece(turn, part, off, *back, True).wait()
+            high, low = two_parts(brecv[turn, part].reshape(rows, lanes))
+            out = bdot(jnp.concatenate([high, low], axis=0), hot_t_ref[...])
+            out = out[:rows] + out[rows:]
+            run_re = run_re + jnp.sum(ta_ref[part] * out, axis=0, keepdims=True)
+            run_im = run_im + jnp.sum(tb_ref[part] * out, axis=0, keepdims=True)
+            return run_re, run_im
+
+        run_re, run_im = lax.fori_loop(0, chunks, take, (start[0:1], start[1:2]))
+        return jnp.concatenate([run_re, run_im], axis=0)
+
+    def as_row(values):
+        total = jnp.sum(jnp.sum(values, axis=0, keepdims=True), axis=1, keepdims=True)
+        return jnp.broadcast_to(total, (1, 128))
+
+    row_count = gsend.shape[1]
+
+    def gram_sums(turn, basis, pair_list):
+        found_rows = []
+        for one, two, use_kin in pair_list:
+            product = basis[one] * basis[two]
+            found_rows.append(as_row(product * kin if use_kin else product))
+        found_rows += [jnp.zeros((1, 128), jnp.float32)] * (row_count - len(found_rows))
+        all_sum(jnp.concatenate(found_rows, axis=0), gsend, grecv, gs_sem, gr_sem, turn)
+        summed = all_sum_end(gsend, grecv, gs_sem, gr_sem, turn) * (1.0 / total_pw)
+        found = {}
+        for slot, (one, two, use_kin) in enumerate(pair_list):
+            value = summed[slot:slot + 1]
+            found[use_kin, one, two] = value
+            found[use_kin, two, one] = value
+        return found
+
+    def realize(coef_map, basis):
+        running = 0.0
+        for index, coef in coef_map.items():
+            running = running + (basis[index] if isinstance(coef, float) and coef == 1.0 else spread_row(coef) * basis[index])
+        return running
+
+    def spread_row(coef):
+        return coef if isinstance(coef, float) else coef[:, 0:1]
+
+    def smooth(residual, level):
+        ratio = kin / (1.5 * level[:, 0:1] + 1.0)
+        poly = 27.0 + ratio * (18.0 + ratio * (12.0 + 8.0 * ratio))
+        square = ratio * ratio
+        return residual * (poly / (poly + 16.0 * square * square))
+
+    coeffs = coeffs_ref[...]
+    h_zero = apply_h(0, coeffs)
+    basis = [coeffs, h_zero]
+    gram = gram_sums(0, basis, new_pairs(0, 2, (False, True)))
+    psi = {0: 1.0}
+    ham = {1: 1.0}
+    eps_zero = gram_form(gram, psi, ham, False) / (gram_form(gram, psi, psi, False) + small_eps)
+    r_map = combine([(1.0, ham), (-eps_zero, psi)])
+    level = gram_form(gram, r_map, r_map, True) / (gram_form(gram, r_map, r_map, False) + small_eps)
+    p_zero = smooth(realize(r_map, basis), level)
+    g_zero = apply_h(1, p_zero)
+    basis += [p_zero, g_zero]
+    gram.update(gram_sums(1, basis, new_pairs(2, 4, (False, True))))
+    q_map = combine([(1.0, {3: 1.0}), (-eps_zero, {2: 1.0})])
+    lam_zero = -gram_form(gram, r_map, q_map, False) / (gram_form(gram, q_map, q_map, False) + small_eps)
+    psi_one = combine([(1.0, psi), (lam_zero, {2: 1.0})])
+    h_one = combine([(1.0, ham), (lam_zero, {3: 1.0})])
+    eps_one = gram_form(gram, psi_one, h_one, False) / (gram_form(gram, psi_one, psi_one, False) + small_eps)
+    r_one = combine([(1.0, h_one), (-eps_one, psi_one)])
+    change = combine([(1.0, r_map), (-1.0, r_one)])
+    weight = gram_form(gram, r_map, change, False) / (gram_form(gram, change, change, False) + small_eps)
+    step = weight * lam_zero
+    psi_mid = combine([(1.0, psi), (step, {2: 1.0})])
+    h_mid = combine([(1.0, ham), (step, {3: 1.0})])
+    r_mid = combine([(1.0, r_map), (-weight, change)])
+    eps_mid = gram_form(gram, psi_mid, h_mid, False) / (gram_form(gram, psi_mid, psi_mid, False) + small_eps)
+    level = gram_form(gram, r_mid, r_mid, True) / (gram_form(gram, r_mid, r_mid, False) + small_eps)
+    p_one = smooth(realize(r_mid, basis), level)
+    g_one = apply_h(2, p_one)
+    basis += [p_one, g_one]
+    gram.update(gram_sums(2, basis, new_pairs(4, 6, (False,))))
+    q_one = combine([(1.0, {5: 1.0}), (-eps_mid, {4: 1.0})])
+    lam_one = -gram_form(gram, r_mid, q_one, False) / (gram_form(gram, q_one, q_one, False) + small_eps)
+    new_map = combine([(1.0, psi_mid), (lam_one, {4: 1.0})])
+    ham_new = combine([(1.0, h_mid), (lam_one, {5: 1.0})])
+    norm_new = gram_form(gram, new_map, new_map, False) + small_eps
+    energy = gram_form(gram, new_map, ham_new, False) / norm_new
+    resid = combine([(1.0, ham_new), (-energy, new_map)])
+    resid_norm = gram_form(gram, resid, resid, False) / norm_new
+    new = realize(new_map, basis)
+    new_h = realize(ham_new, basis)
+    new_ref[...] = new
+    both = jnp.concatenate([new, new_h, jnp.zeros((4, pw), jnp.float32)], axis=0)
+    nsend[...] = both
+    nrecv[band] = both
+
+    def swap(off, incoming):
+        source = lax.rem(band + bands - off, bands) if incoming else band
+        return pltpu.make_async_remote_copy(
+            src_ref=nsend, dst_ref=nrecv.at[source], send_sem=ns_sem.at[off - 1], recv_sem=nr_sem.at[off - 1],
+            device_id={"band": lax.rem(band + off, bands)}, device_id_type=MESH)
+
+    for off in range(1, bands):
+        swap(off, False).start()
+    for off in range(1, bands):
+        swap(off, True).wait()
+    found_rows = []
+    for first in (0, 2):
+        for imag in (False, True):
+            for other in range(bands):
+                o_re = nrecv[other, first:first + 1]
+                o_im = nrecv[other, first + 1:first + 2]
+                if imag:
+                    found_rows.append(as_row(new[0:1] * o_im - new[1:2] * o_re))
+                else:
+                    found_rows.append(as_row(new[0:1] * o_re + new[1:2] * o_im))
+    all_sum(jnp.concatenate(found_rows, axis=0), csend, crecv, cs_sem, cr_sem, 0)
+    summed = all_sum_end(csend, crecv, cs_sem, cr_sem, 0) * (1.0 / total_pw)
+    scal_ref[...] = jnp.concatenate([summed, energy, resid_norm, jnp.zeros((6, 128), jnp.float32)], axis=0)
+
+
+def kernel_body(coeffs, cell_map, potential, projectors, strengths, proj_atom, proj_chan):
+    group = lax.axis_size("ga")
+    bands = lax.axis_size("band")
+    grid_len = potential.shape[0]
+    planes = grid_len // group
+    chunks = planes // QUAD
+    pw = coeffs.shape[2]
+    total_pw = pw * group
+    device = lax.axis_index("ga")
+    plane_num = cell_map // (grid_len * grid_len)
+    y_index = cell_map // grid_len % grid_len
+    z_index = cell_map % grid_len
+    freq_x = signed_freq(device + group * plane_num, grid_len)
+    freq_y = signed_freq(y_index, grid_len)
+    freq_z = signed_freq(z_index, grid_len)
+    kinetic = kin_unit * (freq_x * freq_x + freq_y * freq_y + freq_z * freq_z).astype(jnp.float32)
+    key = plane_num * grid_len + z_index
+    pot = (potential * (1.0 / grid_len**3)).reshape(group, 4, TRIPLE, chunks, QUAD, grid_len)
+    pot = jnp.transpose(pot, (3, 0, 4, 2, 1, 5)).reshape(chunks, group, 1, QUAD, planes * grid_len)
+    rows = group * 2 * QUAD
+    lanes = planes * grid_len
+    pot = jnp.broadcast_to(pot, (chunks, group, 2, QUAD, lanes)).reshape(chunks, rows, lanes)
+    coupling = coupling_matrix(proj_atom, proj_chan, strengths)
+    blank = jnp.zeros_like(coupling)
+    coup = jnp.stack([
+        jnp.block([[coupling, blank], [blank, coupling]]),
+        jnp.block([[blank, -coupling], [coupling, blank]]),
+    ])
+    proj_rows = 2 * projectors.shape[1]
+    tables = [jnp.asarray(t) for t in const_tables(grid_len, group)]
+    gram_rows = 16
+    piece_shape = (3, chunks, group, 2 * QUAD, lanes)
+    dma = pltpu.SemaphoreType.DMA
+    vmem = pl.BlockSpec(memory_space=pltpu.VMEM)
+    f32 = jnp.float32
+    new, scal = pl.pallas_call(
+        functools.partial(sweep_kernel, (group, bands, chunks, grid_len, total_pw, pw)),
+        out_shape=(
+            jax.ShapeDtypeStruct((2, pw), f32),
+            jax.ShapeDtypeStruct((4 * bands + 8, 128), f32),
+        ),
+        in_specs=[vmem] * 13,
+        out_specs=(vmem, vmem),
+        scratch_shapes=[
+            pltpu.VMEM((pw, lanes), jnp.bfloat16),
+            pltpu.VMEM((lanes, pw), jnp.bfloat16),
+            pltpu.VMEM((chunks, rows, pw), f32),
+            pltpu.VMEM((chunks, rows, pw), f32),
+            pltpu.VMEM(piece_shape, f32),
+            pltpu.VMEM(piece_shape, f32),
+            pltpu.VMEM(piece_shape, f32),
+            pltpu.VMEM(piece_shape, f32),
+            pltpu.VMEM((3, 2, proj_rows), f32),
+            pltpu.VMEM((3, group, 2, proj_rows), f32),
+            pltpu.VMEM((3, gram_rows, 128), f32),
+            pltpu.VMEM((3, group, gram_rows, 128), f32),
+            pltpu.VMEM((8, pw), f32),
+            pltpu.VMEM((bands, 8, pw), f32),
+            pltpu.VMEM((1, 4 * bands, 128), f32),
+            pltpu.VMEM((1, group, 4 * bands, 128), f32),
+            dma((3, chunks, group - 1)), dma((3, chunks, group - 1)),
+            dma((3, chunks, group - 1)), dma((3, chunks, group - 1)),
+            dma((3, group - 1)), dma((3, group - 1)),
+            dma((3, group - 1)), dma((3, group - 1)),
+            dma((bands - 1,)), dma((bands - 1,)),
+            dma((1, group - 1)), dma((1, group - 1)),
+        ],
+        compiler_params=pltpu.CompilerParams(
+            collective_id=0, has_side_effects=True, vmem_limit_bytes=60 * 1024 * 1024
+        ),
+        name="sweeps",
+    )(
+        coeffs.reshape(2, pw), kinetic[None, :], y_index[None, :], key[None, :], key[:, None],
+        pot, projectors.reshape(proj_rows, pw), coup, *tables,
+    )
+    rows_out = scal[: 4 * bands, 0].reshape(2, 2, 1, bands)
+    return (
+        new.reshape(2, 1, pw), scal[4 * bands, :1], scal[4 * bands + 1, :1], rows_out[0], rows_out[1],
+    )
+
+
+def body(coeffs, cell_map, potential, projectors, strengths, proj_atom, proj_chan):
+    group = lax.axis_size("ga")
+    grid_len = potential.shape[0]
+    planes = grid_len // group
+    fits = (
+        planes == 4 * TRIPLE
+        and 4 * grid_len % 128 == 0
+        and coeffs.shape[1] == 1
+        and coeffs.shape[2] % 256 == 0
+        and 2 * projectors.shape[1] == 128
+    )
+    chosen = kernel_body if fits else plain_body
+    return chosen(coeffs, cell_map, potential, projectors, strengths, proj_atom, proj_chan)
+
+
 def solution(mesh):
     placed = (
         P(None, "band", "ga"),

time: 588 us -> 124 us (0.21); the launches traced: 577 us -> 123 us
  local copies, waits for them, and re-layouts: 225 us -> 12.9 us
  blocking collectives: 136 us -> 0 us
  Pallas kernels: 0 us -> 103 us
  between operations: 72.1 us -> 0.73 us
  matrix products: 72.4 us -> 2.83 us
  waiting for transfers between devices: 36.9 us -> 0 us
  starting transfers between devices: 24.2 us -> 0 us
  other arithmetic: 10.1 us -> 3.26 us
    psum x7 -> x0, blocking collectives: 110 us -> none  [the longest x3 62.5 us: projected_part(): proj_re, proj_im = lax.psum((proj_re, proj_im), 'ga')]
    pallas_call x0 -> x1, Pallas kernels: none -> 103 us  [kernel_body(): pl.pallas_call(functools.partial(sweep_kernel, (group, bands, chunks, gri...]
    gather x6 -> x0, local copies, waits for them, and re-layouts: 73.9 us -> none  [local_part(): return jnp.stack([flat_grid[:, slot_re], flat_grid[:, slot_im]])]
    dot_general x68 -> x0, matrix products: 71.8 us -> none  [the longest x12 26.6 us: mix_dim(): direct = jnp.einsum(pattern, cos_table, grid_vals, precision=top_precision)]
    scatter x6 -> x0, local copies, waits for them, and re-layouts: 56.4 us -> none  [local_part(): flat_grid.at[:, slot_re].set(vectors[0]).at[:, slot_im].set(vectors[1])]
    all_to_all x6 -> x0, waiting for transfers between devices: 36.9 us -> none  [the longest x3 36.9 us: real_space(): lax.all_to_all(grid_vals, 'ga', split_axis=1, concat_axis=2, tiled=True)]
    another operation x27 -> x0, local copies, waits for them, and re-layouts: 32.5 us -> none  [the longest x3 19.8 us: gram_sums(): summed = lax.psum(jnp.stack(stacked), 'ga') / total_pw]
    all_gather x2 -> x0, blocking collectives: 26.6 us -> none  [the longest x1 13.4 us: body(): piece_ham = lax.all_gather(new_ham, 'band', axis=1, tiled=True)]
  transfers between devices with their start and end apart: 6 -> 0, of which waited for: 3 -> 0; matrix products, arithmetic and copies ran while one was open for 3% -> 0% of each run, Pallas kernels for 0% -> 0%
where the time goes in v1:
time: 124 us; the launch traced here: 123 us
  Pallas kernels  103 us (83%)
  local copies, waits for them, and re-layouts  12.9 us (10%)
  other arithmetic  3.26 us (3%)
  matrix products  2.83 us (2%)
    pallas_call x1, Pallas kernels, kernel_body(): pl.pallas_call(functools.partial(sweep_kernel, (group, bands, chunks, gri...  103 us
    unnamed x5, local copies, waits for them, and re-layouts  3.52 us

profile of v1, /device:TPU:0, one launch (start us, length us, event | category | flops | bytes accessed | tf_op | source)
XLA Modules:
  0.0 123.0 jit_solution(3981484870744705628)
XLA Ops:
  0.6 0.0 copy-start
  0.6 0.8 fusion.15
  1.5 0.6 broadcast_in_dim.24.kin_ref
  2.1 1.3 %copy.36 = f32[2,1,2304]{2,0,1:T(2,128)} copy(f32[2,1,2304]{2,1,0:T(1,128)} %param.12) | data formatting | bytes 36864
  3.4 0.7 multiply_add_fusion
  4.1 0.6 broadcast_in_dim.25.ynum_ref
  4.7 0.6 broadcast_in_dim.26.key_row_ref
  5.3 0.8 copy.24
  6.2 0.9 fusion.6
  7.1 0.8 fusion.4
  7.9 0.1 broadcast_multiply_fusion.1
  8.0 0.1 copy.29
  8.1 1.0 convolution_bitcast_fusion
  9.1 0.9 fusion.21
  10.1 0.1 fusion.1
  10.1 0.7 pad_maximum_fusion.coup_ref
  10.8 0.0 copy-done
  10.8 0.1 broadcast_multiply_fusion
  10.9 0.3 reshape.39
  11.1 0.2 copy.32
  11.3 0.5 reshape.40
  11.8 0.1 broadcast_in_dim.29
  11.9 1.3 %reshape.35.pot_ref = f32[3,64,1152]{2,1,0:T(8,128)} reshape(f32[3,8,2,4,1152]{4,3,2,1,0:T(4,128)S(1)} %broadcast_in_dim.29) | data formatting | bytes 1769472 | tf_op jit(solution)/shard_map/reshape | solution.py:663
  13.2 1.8 %broadcast_in_dim.30.key_col_ref = s32[2304,1]{1,0:T(8,128)} reshape(s32[2304]{0:T(1024)S(1)} %get-tuple-element.25) | data formatting | bytes 18432 | tf_op jit(solution)/shard_map/broadcast_in_dim | solution.py:714
  15.0 103.2 %sweeps.1 = (f32[2,2304]{1,0:T(2,128)}, f32[24,128]{1,0:T(8,128)}) custom-call(f32[2,2304]{1,0:T(2,128)} %bitcast.28, f32[1,2304]{1,0:T(1,128)} %broadcast_in_dim.24.kin_ref, s32[1,2304]{1,0:T(1,128)} %broadcast_in_dim.25.ynum_ref, s32[1,2304]{1,0:T(1,128)} %broadcast_in_dim.26.key_row_ref, s32[2304,1]{1,0:T(8,128)} %broadcast_in_dim.30.key_col_ref, ...), custom_call_target="tpu_custom_call" | custom-call | tf_op jit(solution)/shard_map/sweeps/pallas_call | solution.py:677
  118.2 1.3 %copy.26 = f32[2,1,2304]{2,1,0:T(1,128)} copy(f32[2,1,2304]{2,0,1:T(2,128)} %bitcast.29) | data formatting | bytes 36864
  119.6 1.3 %fusion.20 = (f32[1,1]{1,0:T(1,128)}, f32[1,1]{1,0:T(1,128)}) fusion(f32[24,128]{1,0:T(8,128)} %get-tuple-element.8), kind=kLoop, calls=%fused_computation.45 | loop fusion | bytes 16 | tf_op jit(solution)/shard_map/slice | solution.py:719
  120.9 0.8 slice_reduce_fusion
  121.7 0.7 squeeze.15
  122.3 0.6 squeeze.14
  (1 shorter events, 0.0 us)
Async XLA Ops:
  0.6 10.2 %copy-start = (f32[96,12,96]{2,0,1:T(8,128)S(1)}, f32[96,12,96]{2,0,1:T(8,128)}, u32[]{:S(2)}) copy-start(f32[96,12,96]{2,0,1:T(8,128)} %param.14) | copy-start | bytes 1327108

commit v2 on v1

--- a/solution.py
+++ b/solution.py
@@ -365,10 +365,10 @@
 
 def sweep_kernel(
     dims,
-    coeffs_ref, kin_ref, ynum_ref, key_row_ref, key_col_ref, pot_ref, proj_ref, coup_ref,
+    coeffs_ref, cell_ref, potential_ref, proj_ref, strength_ref, atom_ref, chan_ref,
     wave_ref, fourz_ref, across_ref, lane_ref, dev_ref,
     new_ref, scal_ref,
-    hot_ref, hot_t_ref, ta_ref, tb_ref,
+    hot_ref, hot_t_ref, ta_ref, tb_ref, key_ref, pot_ref,
     fsend, frecv, bsend, brecv, psend, precv, gsend, grecv, nsend, nrecv, csend, crecv,
     fs_sem, fr_sem, bs_sem, br_sem, ps_sem, pr_sem, gs_sem, gr_sem, ns_sem, nr_sem, cs_sem, cr_sem,
 ):
@@ -385,33 +385,75 @@
     for off in range(1, bands):
         pl.semaphore_signal(barrier, inc=1, device_id={"band": lax.rem(band + off, bands)}, device_id_type=MESH)
 
-    hot_rows = 256
+    def whole(values):
+        return jnp.floor(values)
+
+    cell = cell_ref[...].astype(jnp.float32)
+    plane = whole((cell + 0.5) * (1.0 / (grid_len * grid_len)))
+    in_plane = cell - plane * (grid_len * grid_len)
+    y_num = whole((in_plane + 0.5) * (1.0 / grid_len))
+    z_num = in_plane - y_num * grid_len
+    key_ref[...] = plane * grid_len + z_num
+
+    def signed(values):
+        return jnp.where(2.0 * values < grid_len, values, values - grid_len)
+
+    f_x = signed(plane * group + me.astype(jnp.float32))
+    f_y, f_z = signed(y_num), signed(z_num)
+    kin = kin_unit * (f_x * f_x + f_y * f_y + f_z * f_z)
 
     def build_hot(step, carry):
-        at = pl.multiple_of(step * hot_rows, hot_rows)
-        lane_id = lax.broadcasted_iota(jnp.int32, (hot_rows, lanes), 1)
-        hot_ref[pl.ds(at, hot_rows), :] = (lane_id == key_col_ref[pl.ds(at, hot_rows), :]).astype(jnp.float32).astype(jnp.bfloat16)
+        at = pl.multiple_of(step * 128, 128)
+        key_col = jnp.transpose(jnp.broadcast_to(key_ref[:, pl.ds(at, 128)], (128, 128)))
+        lane_id = lax.broadcasted_iota(jnp.int32, (128, 128), 1).astype(jnp.float32)
+        for k in range(lanes // 128):
+            hit = jnp.where(lane_id == key_col - 128.0 * k, 1.0, 0.0)
+            hot_ref[pl.ds(at, 128), k * 128:(k + 1) * 128] = hit.astype(jnp.bfloat16)
         return carry
 
-    lax.fori_loop(0, pw // hot_rows, build_hot, 0)
-    turn_rows = 128
-
-    def build_turn(step, carry):
-        at = pl.multiple_of(step * turn_rows, turn_rows)
-        row_id = lax.broadcasted_iota(jnp.int32, (turn_rows, pw), 0) + at
-        hot_t_ref[pl.ds(at, turn_rows), :] = (row_id == key_row_ref[...]).astype(jnp.float32).astype(jnp.bfloat16)
-        return carry
-
-    lax.fori_loop(0, lanes // turn_rows, build_turn, 0)
-    y_hot = (lax.broadcasted_iota(jnp.int32, (grid_len, pw), 0) == ynum_ref[...]).astype(jnp.float32).astype(jnp.bfloat16)
+    lax.fori_loop(0, pw // 128, build_hot, 0)
+    y_hot = jnp.where(lax.broadcasted_iota(jnp.int32, (grid_len, pw), 0).astype(jnp.float32) == y_num, 1.0, 0.0).astype(jnp.bfloat16)
     for part in range(chunks):
         for table, base in ((ta_ref, 0), (tb_ref, chunks * rows)):
             at = base + part * rows
             table[part] = bdot(wave_ref[0, at:at + rows, :], y_hot) + bdot(wave_ref[1, at:at + rows, :], y_hot)
 
+    def build_turn():
+        turn_rows = 128
+
+        def step_turn(step, carry):
+            at = pl.multiple_of(step * turn_rows, turn_rows)
+            row_id = (lax.broadcasted_iota(jnp.int32, (turn_rows, pw), 0) + at).astype(jnp.float32)
+            hot_t_ref[pl.ds(at, turn_rows), :] = jnp.where(row_id == key_ref[...], 1.0, 0.0).astype(jnp.bfloat16)
+            return carry
+
+        lax.fori_loop(0, lanes // turn_rows, step_turn, 0)
+
+    def build_potential():
+        for part in range(chunks):
+            for b in range(TRIPLE):
+                for a in range(4):
+                    at = (b * 4 + a) * grid_len
+                    block = potential_ref[:, TRIPLE * a + b, part * QUAD:(part + 1) * QUAD, :] * (1.0 / grid_len**3)
+                    pot_ref[part, :, :QUAD, at:at + grid_len] = block
+                    pot_ref[part, :, QUAD:, at:at + grid_len] = block
+
+    def build_coupling():
+        atoms, chans = strength_ref.shape[0] // strength_ref.shape[1], strength_ref.shape[1]
+        size = atoms * chans
+        ident = atom_ref[...] * chans + chan_ref[...]
+        hot = (lax.broadcasted_iota(jnp.int32, (size, ident.shape[1]), 0) == ident).astype(jnp.float32)
+        row_at = lax.broadcasted_iota(jnp.int32, (size, size), 0)
+        col_at = lax.broadcasted_iota(jnp.int32, (size, size), 1)
+        tiled = jnp.concatenate([strength_ref[...]] * atoms, axis=1)
+        same = (row_at // chans == col_at // chans).astype(jnp.float32)
+        block = tiled * same
+        block = 0.5 * (block + jnp.transpose(block))
+        half = lax.dot_general(hot, block, (((0,), (0,)), ((), ())), precision=top_precision, preferred_element_type=jnp.float32)
+        return jnp.dot(half, hot, precision=top_precision, preferred_element_type=jnp.float32)
+
     pl.semaphore_wait(barrier, group + bands - 2)
 
-    kin = kin_ref[...]
     sign = jnp.where(lax.broadcasted_iota(jnp.int32, (1, 2 * QUAD, 1), 1) < QUAD, -1.0, 1.0).astype(jnp.float32)
 
     def times_i(values):
@@ -494,13 +536,17 @@
         lax.fori_loop(0, chunks, put, 0)
         sums = lax.dot_general(vector, proj_ref[...], (((1,), (1,)), ((), ())), precision=top_precision, preferred_element_type=jnp.float32)
         all_sum(sums, psend, precv, ps_sem, pr_sem, turn)
+        if turn == 0:
+            build_potential()
+            shared.append(build_coupling())
+            build_turn()
 
         def middle(part, carry):
             for off in range(1, group):
                 piece(turn, part, off, *fwd, True).wait()
             triple = turn_lane(three(lane_split(frecv[turn, part]), 1.0), 1.0)
             values = turn_dev(jnp.concatenate(mix_fourz(triple, 1.0), axis=-1), 1.0)
-            values = mix_devices(values, 0) * pot_ref[part]
+            values = mix_devices(values, 0) * pot_ref[part].reshape(rows, lanes)
             values = mix_devices(values, 1).reshape(group, 2 * QUAD, lanes)
             triple = mix_fourz(lane_split(turn_dev(values, -1.0)), -1.0)
             triple = three(turn_lane(triple, -1.0), -1.0)
@@ -512,9 +558,13 @@
 
         lax.fori_loop(0, chunks, middle, 0)
         sums = all_sum_end(psend, precv, ps_sem, pr_sem, turn) * (1.0 / total_pw)
-        direct = jnp.dot(sums, coup_ref[0], precision=top_precision, preferred_element_type=jnp.float32)
-        turned = jnp.dot(sums, coup_ref[1], precision=top_precision, preferred_element_type=jnp.float32)
-        weights = jnp.concatenate([direct[0:1] + turned[1:2], direct[1:2] - turned[0:1]], axis=0)
+        half = sums.shape[1] // 2
+        pair = jnp.concatenate([
+            sums[0:1, :half] + sums[1:2, half:], sums[1:2, :half] - sums[0:1, half:]], axis=0)
+        mixed = jnp.dot(pair, shared[0], precision=top_precision, preferred_element_type=jnp.float32)
+        m_re, m_im = mixed[0:1], mixed[1:2]
+        weights = jnp.concatenate([
+            jnp.concatenate([m_re, -m_im], axis=1), jnp.concatenate([m_im, m_re], axis=1)], axis=0)
         nonlocal_part = jnp.dot(weights, proj_ref[...], precision=top_precision, preferred_element_type=jnp.float32)
         start = kin * vector + nonlocal_part
 
@@ -568,7 +618,8 @@
         square = ratio * ratio
         return residual * (poly / (poly + 16.0 * square * square))
 
-    coeffs = coeffs_ref[...]
+    shared = []
+    coeffs = coeffs_ref[:, 0, :]
     h_zero = apply_h(0, coeffs)
     basis = [coeffs, h_zero]
     gram = gram_sums(0, basis, new_pairs(0, 2, (False, True)))
@@ -639,6 +690,20 @@
     scal_ref[...] = jnp.concatenate([summed, energy, resid_norm, jnp.zeros((6, 128), jnp.float32)], axis=0)
 
 
+def finish_kernel(bands, new_ref, scal_ref, bands_ref, energy_ref, norm_ref, corr_ref, sub_ref):
+    bands_ref[:, 0, :] = new_ref[...]
+    lane = lax.broadcasted_iota(jnp.int32, (1, bands), 1)
+    for ref, base in ((corr_ref, 0), (sub_ref, 2 * bands)):
+        for part in range(2):
+            row = jnp.zeros((1, bands), jnp.float32)
+            for other in range(bands):
+                at = base + part * bands + other
+                row = jnp.where(lane == other, scal_ref[at:at + 1, :bands], row)
+            ref[part] = row
+    energy_ref[0] = scal_ref[4 * bands, 0]
+    norm_ref[0] = scal_ref[4 * bands + 1, 0]
+
+
 def kernel_body(coeffs, cell_map, potential, projectors, strengths, proj_atom, proj_chan):
     group = lax.axis_size("ga")
     bands = lax.axis_size("band")
@@ -647,26 +712,8 @@
     chunks = planes // QUAD
     pw = coeffs.shape[2]
     total_pw = pw * group
-    device = lax.axis_index("ga")
-    plane_num = cell_map // (grid_len * grid_len)
-    y_index = cell_map // grid_len % grid_len
-    z_index = cell_map % grid_len
-    freq_x = signed_freq(device + group * plane_num, grid_len)
-    freq_y = signed_freq(y_index, grid_len)
-    freq_z = signed_freq(z_index, grid_len)
-    kinetic = kin_unit * (freq_x * freq_x + freq_y * freq_y + freq_z * freq_z).astype(jnp.float32)
-    key = plane_num * grid_len + z_index
-    pot = (potential * (1.0 / grid_len**3)).reshape(group, 4, TRIPLE, chunks, QUAD, grid_len)
-    pot = jnp.transpose(pot, (3, 0, 4, 2, 1, 5)).reshape(chunks, group, 1, QUAD, planes * grid_len)
     rows = group * 2 * QUAD
     lanes = planes * grid_len
-    pot = jnp.broadcast_to(pot, (chunks, group, 2, QUAD, lanes)).reshape(chunks, rows, lanes)
-    coupling = coupling_matrix(proj_atom, proj_chan, strengths)
-    blank = jnp.zeros_like(coupling)
-    coup = jnp.stack([
-        jnp.block([[coupling, blank], [blank, coupling]]),
-        jnp.block([[blank, -coupling], [coupling, blank]]),
-    ])
     proj_rows = 2 * projectors.shape[1]
     tables = [jnp.asarray(t) for t in const_tables(grid_len, group)]
     gram_rows = 16
@@ -680,13 +727,15 @@
             jax.ShapeDtypeStruct((2, pw), f32),
             jax.ShapeDtypeStruct((4 * bands + 8, 128), f32),
         ),
-        in_specs=[vmem] * 13,
+        in_specs=[vmem] * 12,
         out_specs=(vmem, vmem),
         scratch_shapes=[
             pltpu.VMEM((pw, lanes), jnp.bfloat16),
             pltpu.VMEM((lanes, pw), jnp.bfloat16),
             pltpu.VMEM((chunks, rows, pw), f32),
             pltpu.VMEM((chunks, rows, pw), f32),
+            pltpu.VMEM((1, pw), f32),
+            pltpu.VMEM((chunks, group, 2 * QUAD, lanes), f32),
             pltpu.VMEM(piece_shape, f32),
             pltpu.VMEM(piece_shape, f32),
             pltpu.VMEM(piece_shape, f32),
@@ -711,13 +760,25 @@
         ),
         name="sweeps",
     )(
-        coeffs.reshape(2, pw), kinetic[None, :], y_index[None, :], key[None, :], key[:, None],
-        pot, projectors.reshape(proj_rows, pw), coup, *tables,
-    )
-    rows_out = scal[: 4 * bands, 0].reshape(2, 2, 1, bands)
-    return (
-        new.reshape(2, 1, pw), scal[4 * bands, :1], scal[4 * bands + 1, :1], rows_out[0], rows_out[1],
-    )
+        coeffs, cell_map.reshape(1, pw), potential.reshape(group, planes, planes, grid_len),
+        projectors.reshape(proj_rows, pw), strengths.reshape(-1, strengths.shape[2]),
+        proj_atom.reshape(1, -1), proj_chan.reshape(1, -1), *tables,
+    )
+
+    smem = pl.BlockSpec(memory_space=pltpu.SMEM)
+    return pl.pallas_call(
+        functools.partial(finish_kernel, bands),
+        out_shape=(
+            jax.ShapeDtypeStruct((2, 1, pw), f32),
+            jax.ShapeDtypeStruct((1,), f32),
+            jax.ShapeDtypeStruct((1,), f32),
+            jax.ShapeDtypeStruct((2, 1, bands), f32),
+            jax.ShapeDtypeStruct((2, 1, bands), f32),
+        ),
+        in_specs=[vmem, vmem],
+        out_specs=(vmem, smem, smem, vmem, vmem),
+        name="finish",
+    )(new, scal)
 
 
 def body(coeffs, cell_map, potential, projectors, strengths, proj_atom, proj_chan):

time: 124 us -> 109 us (0.88)
  local copies, waits for them, and re-layouts: 12.9 us -> 3.61 us
  other arithmetic: 3.26 us -> 0 us
  matrix products: 2.83 us -> 0 us
    broadcast_in_dim x7 -> x0, local copies, waits for them, and re-layouts: 4.36 us -> none  [the longest x1 1.83 us: kernel_body(): key[:, None]]
    dot_general x3 -> x0, matrix products: 2.83 us -> none  [the longest x1 1.01 us: coupling_matrix(): jnp.einsum('pa,pc,acd->pd', atom_hot, chan_hot, symmetric, precision=top_...]
    slice x2 -> x0, local copies, waits for them, and re-layouts: 2.1 us -> none  [the longest x1 1.27 us: kernel_body(): scal[4 * bands + 1, :1]]
    another operation x3 -> x0, other arithmetic: 1.53 us -> none  [the longest x2 0.77 us: kernel_body(): jnp.stack([jnp.block([[coupling, blank], [blank, coupling]]), jnp.block([...]
    pallas_call x0 -> x1, Pallas kernels: none -> 1.36 us  [kernel_body(): pl.pallas_call(functools.partial(finish_kernel, bands), out_shape=(jax.Sh...]
    squeeze x2 -> x0, local copies, waits for them, and re-layouts: 1.29 us -> none  [the longest x1 0.65 us: kernel_body(): rows_out[1]]
    unnamed x5 -> x1, local copies, waits for them, and re-layouts: 3.52 us -> 2.3 us
where the time goes in v2:
time: 109 us
  Pallas kernels  104 us (95%)
  local copies, waits for them, and re-layouts  3.61 us (3%)
    pallas_call x1, Pallas kernels, kernel_body(): pl.pallas_call(functools.partial(sweep_kernel, (group, bands, chunks, gri...  103 us
    unnamed x1, local copies, waits for them, and re-layouts  2.3 us

profile of v2, /device:TPU:0, one launch (start us, length us, event | category | flops | bytes accessed | tf_op | source)
XLA Modules:
  0.0 108.9 jit_solution(16663809690613395014)
XLA Ops:
  0.6 1.3 %reshape.28.cell_ref = s32[1,2304]{1,0:T(1,128)} reshape(s32[2304]{0:T(1024)} %param.13) | data formatting | bytes 18432 | tf_op jit(solution)/shard_map/reshape | solution.py:763
  1.9 2.3 %copy.17 = f32[96,12,96]{2,1,0:T(8,128)} copy(f32[96,12,96]{2,0,1:T(8,128)} %param.14) | data formatting | bytes 884736 | tf_op args[2]
  4.2 103.1 %sweeps.1 = (f32[2,2304]{1,0:T(2,128)}, f32[24,128]{1,0:T(8,128)}) custom-call(f32[2,1,2304]{2,1,0:T(1,128)} %coeffs_ref.1, s32[1,2304]{1,0:T(1,128)} %reshape.28.cell_ref, f32[8,12,12,96]{3,2,1,0:T(8,128)} %bitcast.5, f32[128,2304]{1,0:T(8,128)} %bitcast.6, f32[64,8]{1,0:T(8,128)} %bitcast.7, s32[1,64]{1,0:T(1,128)} %bitcast.8, s32[1,64]{1,0:T(1,128)} %bitcast.9, ...), custom_call_target="tpu_custom_call" | custom-call | tf_op jit(solution)/shard_map/sweeps/pallas_call | solution.py:724
  107.4 1.4 %finish.1 = (f32[2,1,2304]{2,1,0:T(1,128)}, f32[1]{0:T(128)}, f32[1]{0:T(128)}, f32[2,1,4]{2,1,0:T(1,128)}, f32[2,1,4]{2,1,0:T(1,128)}) custom-call(f32[2,2304]{1,0:T(2,128)} %get-tuple-element.7.new_ref, f32[24,128]{1,0:T(8,128)} %get-tuple-element.8.scal_ref), custom_call_target="tpu_custom_call" | custom-call | tf_op jit(solution)/shard_map/finish/pallas_call | solution.py:769

commit v3 on v2

--- a/solution.py
+++ b/solution.py
@@ -365,11 +365,11 @@
 
 def sweep_kernel(
     dims,
-    coeffs_ref, cell_ref, potential_ref, proj_ref, strength_ref, atom_ref, chan_ref,
-    wave_ref, fourz_ref, across_ref, lane_ref, dev_ref,
+    coeffs_ref, cell_ref, potential_hbm, proj_hbm, strength_ref, atom_ref, chan_ref,
+    wave_ref, fourz_hbm, across_ref, lane_ref, dev_ref,
     new_ref, scal_ref,
-    hot_ref, hot_t_ref, ta_ref, tb_ref, key_ref, pot_ref,
-    fsend, frecv, bsend, brecv, psend, precv, gsend, grecv, nsend, nrecv, csend, crecv,
+    hot_ref, hot_t_ref, ta_ref, tb_ref, key_ref, pot_ref, potential_ref, proj_ref, fourz_ref, in_sem,
+    fsend, frecv, bsend, brecv, psend, precv, gsend, grecv, nsend, nrecv, isend, irecv, lsend, lrecv, csend, crecv,
     fs_sem, fr_sem, bs_sem, br_sem, ps_sem, pr_sem, gs_sem, gr_sem, ns_sem, nr_sem, cs_sem, cr_sem,
 ):
     group, bands, chunks, grid_len, total_pw, pw = dims
@@ -379,6 +379,13 @@
     me = lax.axis_index("ga")
     band = lax.axis_index("band")
 
+    loads = [
+        pltpu.make_async_copy(source, target, in_sem.at[k])
+        for k, (source, target) in enumerate(
+            ((proj_hbm, proj_ref), (potential_hbm, potential_ref), (fourz_hbm, fourz_ref)))
+    ]
+    for load in loads:
+        load.start()
     barrier = pltpu.get_barrier_semaphore()
     for off in range(1, group):
         pl.semaphore_signal(barrier, inc=1, device_id={"ga": lax.rem(me + off, group)}, device_id_type=MESH)
@@ -534,6 +541,9 @@
             return carry
 
         lax.fori_loop(0, chunks, put, 0)
+        if turn == 0:
+            for load in loads:
+                load.wait()
         sums = lax.dot_general(vector, proj_ref[...], (((1,), (1,)), ((), ())), precision=top_precision, preferred_element_type=jnp.float32)
         all_sum(sums, psend, precv, ps_sem, pr_sem, turn)
         if turn == 0:
@@ -647,7 +657,23 @@
     eps_mid = gram_form(gram, psi_mid, h_mid, False) / (gram_form(gram, psi_mid, psi_mid, False) + small_eps)
     level = gram_form(gram, r_mid, r_mid, True) / (gram_form(gram, r_mid, r_mid, False) + small_eps)
     p_one = smooth(realize(r_mid, basis), level)
+
+    def swap(which, send, recv, off, incoming):
+        source = lax.rem(band + bands - off, bands) if incoming else band
+        return pltpu.make_async_remote_copy(
+            src_ref=send, dst_ref=recv.at[source],
+            send_sem=ns_sem.at[which, off - 1], recv_sem=nr_sem.at[which, off - 1],
+            device_id={"band": lax.rem(band + off, bands)}, device_id_type=MESH)
+
+    def share(which, send, recv, values):
+        send[...] = values
+        recv[band] = values
+        for off in range(1, bands):
+            swap(which, send, recv, off, False).start()
+
+    share(0, nsend, nrecv, jnp.stack([realize(psi_mid, basis), p_one, realize(h_mid, basis)]))
     g_one = apply_h(2, p_one)
+    share(1, isend, irecv, g_one)
     basis += [p_one, g_one]
     gram.update(gram_sums(2, basis, new_pairs(4, 6, (False,))))
     q_one = combine([(1.0, {5: 1.0}), (-eps_mid, {4: 1.0})])
@@ -661,26 +687,20 @@
     new = realize(new_map, basis)
     new_h = realize(ham_new, basis)
     new_ref[...] = new
-    both = jnp.concatenate([new, new_h, jnp.zeros((4, pw), jnp.float32)], axis=0)
-    nsend[...] = both
-    nrecv[band] = both
-
-    def swap(off, incoming):
-        source = lax.rem(band + bands - off, bands) if incoming else band
-        return pltpu.make_async_remote_copy(
-            src_ref=nsend, dst_ref=nrecv.at[source], send_sem=ns_sem.at[off - 1], recv_sem=nr_sem.at[off - 1],
-            device_id={"band": lax.rem(band + off, bands)}, device_id_type=MESH)
-
-    for off in range(1, bands):
-        swap(off, False).start()
-    for off in range(1, bands):
-        swap(off, True).wait()
+    share(2, lsend, lrecv, jnp.broadcast_to(lam_one, (8, 128)))
+    for which, send, recv in ((0, nsend, nrecv), (1, isend, irecv), (2, lsend, lrecv)):
+        for off in range(1, bands):
+            swap(which, send, recv, off, True).wait()
     found_rows = []
-    for first in (0, 2):
+    others = []
+    for other in range(bands):
+        lam = lrecv[other, 0:1, 0:1]
+        others.append((nrecv[other, 0] + lam * nrecv[other, 1], nrecv[other, 2] + lam * irecv[other]))
+    for first in (0, 1):
         for imag in (False, True):
             for other in range(bands):
-                o_re = nrecv[other, first:first + 1]
-                o_im = nrecv[other, first + 1:first + 2]
+                o_re = others[other][first][0:1]
+                o_im = others[other][first][1:2]
                 if imag:
                     found_rows.append(as_row(new[0:1] * o_im - new[1:2] * o_re))
                 else:
@@ -720,6 +740,7 @@
     piece_shape = (3, chunks, group, 2 * QUAD, lanes)
     dma = pltpu.SemaphoreType.DMA
     vmem = pl.BlockSpec(memory_space=pltpu.VMEM)
+    far = pl.BlockSpec(memory_space=pl.ANY)
     f32 = jnp.float32
     new, scal = pl.pallas_call(
         functools.partial(sweep_kernel, (group, bands, chunks, grid_len, total_pw, pw)),
@@ -727,7 +748,7 @@
             jax.ShapeDtypeStruct((2, pw), f32),
             jax.ShapeDtypeStruct((4 * bands + 8, 128), f32),
         ),
-        in_specs=[vmem] * 12,
+        in_specs=[vmem, vmem, far, far] + [vmem] * 4 + [far] + [vmem] * 3,
         out_specs=(vmem, vmem),
         scratch_shapes=[
             pltpu.VMEM((pw, lanes), jnp.bfloat16),
@@ -736,6 +757,10 @@
             pltpu.VMEM((chunks, rows, pw), f32),
             pltpu.VMEM((1, pw), f32),
             pltpu.VMEM((chunks, group, 2 * QUAD, lanes), f32),
+            pltpu.VMEM((group, planes, planes, grid_len), f32),
+            pltpu.VMEM((proj_rows, pw), f32),
+            pltpu.VMEM(tables[1].shape, jnp.bfloat16),
+            pltpu.SemaphoreType.DMA((3,)),
             pltpu.VMEM(piece_shape, f32),
             pltpu.VMEM(piece_shape, f32),
             pltpu.VMEM(piece_shape, f32),
@@ -744,15 +769,19 @@
             pltpu.VMEM((3, group, 2, proj_rows), f32),
             pltpu.VMEM((3, gram_rows, 128), f32),
             pltpu.VMEM((3, group, gram_rows, 128), f32),
-            pltpu.VMEM((8, pw), f32),
-            pltpu.VMEM((bands, 8, pw), f32),
+            pltpu.VMEM((3, 2, pw), f32),
+            pltpu.VMEM((bands, 3, 2, pw), f32),
+            pltpu.VMEM((2, pw), f32),
+            pltpu.VMEM((bands, 2, pw), f32),
+            pltpu.VMEM((8, 128), f32),
+            pltpu.VMEM((bands, 8, 128), f32),
             pltpu.VMEM((1, 4 * bands, 128), f32),
             pltpu.VMEM((1, group, 4 * bands, 128), f32),
             dma((3, chunks, group - 1)), dma((3, chunks, group - 1)),
             dma((3, chunks, group - 1)), dma((3, chunks, group - 1)),
             dma((3, group - 1)), dma((3, group - 1)),
             dma((3, group - 1)), dma((3, group - 1)),
-            dma((bands - 1,)), dma((bands - 1,)),
+            dma((3, bands - 1)), dma((3, bands - 1)),
             dma((1, group - 1)), dma((1, group - 1)),
         ],
         compiler_params=pltpu.CompilerParams(

time: 109 us -> 105 us (0.963)
  Pallas kernels: 104 us -> 100 us
    pallas_call x1, Pallas kernels: 103 us -> 98.6 us  [kernel_body(): pl.pallas_call(functools.partial(sweep_kernel, (group, bands, chunks, gri...]
where the time goes in v3:
time: 105 us; the launch traced here: 104 us
  Pallas kernels  100 us (95%)
  local copies, waits for them, and re-layouts  3.61 us (3%)
    pallas_call x1, Pallas kernels, kernel_body(): pl.pallas_call(functools.partial(sweep_kernel, (group, bands, chunks, gri...  98.6 us
    unnamed x1, local copies, waits for them, and re-layouts  2.3 us

profile of v3, /device:TPU:0, one launch (start us, length us, event | category | flops | bytes accessed | tf_op | source)
XLA Modules:
  0.0 104.4 jit_solution(2413052306142160144)
XLA Ops:
  0.6 1.3 %reshape.28.cell_ref = s32[1,2304]{1,0:T(1,128)} reshape(s32[2304]{0:T(1024)} %param.13) | data formatting | bytes 18432 | tf_op jit(solution)/shard_map/reshape | solution.py:792
  1.9 2.3 %copy.17 = f32[96,12,96]{2,1,0:T(8,128)} copy(f32[96,12,96]{2,0,1:T(8,128)} %param.14) | data formatting | bytes 884736 | tf_op args[2]
  4.2 98.6 %sweeps.1 = (f32[2,2304]{1,0:T(2,128)}, f32[24,128]{1,0:T(8,128)}) custom-call(f32[2,1,2304]{2,1,0:T(1,128)} %coeffs_ref.1, s32[1,2304]{1,0:T(1,128)} %reshape.28.cell_ref, f32[8,12,12,96]{3,2,1,0:T(8,128)} %bitcast.5, f32[128,2304]{1,0:T(8,128)} %bitcast.6, f32[64,8]{1,0:T(8,128)} %bitcast.7, s32[1,64]{1,0:T(1,128)} %bitcast.8, s32[1,64]{1,0:T(1,128)} %bitcast.9, ...), custom_call_target="tpu_custom_call" | custom-call | tf_op jit(solution)/shard_map/sweeps/pallas_call | solution.py:745
  102.9 1.4 %finish.1 = (f32[2,1,2304]{2,1,0:T(1,128)}, f32[1]{0:T(128)}, f32[1]{0:T(128)}, f32[2,1,4]{2,1,0:T(1,128)}, f32[2,1,4]{2,1,0:T(1,128)}) custom-call(f32[2,2304]{1,0:T(2,128)} %get-tuple-element.7.new_ref, f32[24,128]{1,0:T(8,128)} %get-tuple-element.8.scal_ref), custom_call_target="tpu_custom_call" | custom-call | tf_op jit(solution)/shard_map/finish/pallas_call | solution.py:798
